TPU v7x, 32 devices: a whole 2x2x4 slice. The times are simulated.
32 devices in a mesh: gx: 4 (over x, core), gy: 4 (over z), gz: 2 (over y).
Axes of the slice: x: 2, y: 2, z: 4, core: 2. Of those that a mesh axis runs over, the one named last changes fastest.
Arguments:
- particle_fields: float32 [20, 262144], P(None, ('gx', 'gy', 'gz')), may hold values from -4 to 4
- step_length: float32 [262144], P(('gx', 'gy', 'gz')), may hold values from 0.1 to 1
- live_mask: int32 [262144], P(('gx', 'gy', 'gz')), may hold values 0 or 1
- dest_cell: int32 [262144], P(('gx', 'gy', 'gz')), may hold values from 0 to 511
- block_counts: int32 [32, 6], P(('gx', 'gy', 'gz')), may hold values from 0 to 12, as said below
- block_lists: int32 [32, 48], P(('gx', 'gy', 'gz')), may hold values from 0 to 87, as said below
Outputs:
- tile_sums: float32 [20, 16384], P(None, ('gx', 'gy', 'gz'))
Inputs may be any that keep to these rules, and one draw needn't show every extreme that they name: `block_counts`: columns are directions in the order x lower, x upper, z lower, z upper, y lower, y upper; a count is at most its section's span (6, 6 or 12) and may be 0; at every section some domain receives full spans from both neighbours. `block_lists`: per domain, 6 entries toward the lower x neighbour, 6 toward the upper, then 2 * 6 for z and 24 for y in the same way; entries are block numbers of the domain's pool at that section. Entries below their direction's count are valid: valid entries of one domain over all sections are distinct, and each names an own block or an appended block that its sender filled. Other entries are arbitrary numbers within the pool.
All inputs are finite; a program needn't handle non-finite values. No bound on the sum of `live_mask` on one device may be relied on, other than what follows from the above.
Results may differ from a plain program's by a relative error of at most 0.0003.
Values sent between devices are 32-bit elements; how exact they have to be, the bound alone decides.
No kernel may reach another device: no remote copies, remote signals or barrier semaphores. Data moves between devices by JAX's collectives and lax.ppermute only.
A program may use at most 64 MiB of HBM per device.

v0:
```python
import jax
import jax.numpy as jnp
from jax import lax
from jax.sharding import PartitionSpec as P

CELLS = 512
CAP_X = 6
CAP_Z = 6
CAP_Y = 12


def padded_2(array, sides, width):
    for axis, dim in sides:
        devices, length = (lax.axis_size(axis), array.shape[dim])
        up = [(i, (i + 1) % devices) for i in range(devices)]
        down = [(j, i) for i, j in up]
        last = lax.slice_in_dim(array, length - width, length, axis=dim)
        initial = lax.slice_in_dim(array, 0, width, axis=dim)
        before = lax.ppermute(last, axis, up)
        after = lax.ppermute(initial, axis, down)
        array = jnp.concatenate([before, array, after], axis=dim)
    return array


def pick_blocks(holding, chosen, toward_lower, toward_upper):
    extent = chosen.shape[0] // 2
    picked = jnp.take(holding, chosen, axis=1)
    position = jnp.arange(2 * extent) % extent
    wanted = jnp.where(jnp.arange(2 * extent) < extent, toward_lower, toward_upper)
    usable = (position < wanted).astype(jnp.float32)
    return picked * usable[None, :, None]


def arrived(padded, extent):
    margin = extent * 128
    lower_part = padded[:, :margin]
    upper_part = padded[:, padded.shape[1] - margin :]
    return jnp.concatenate([lower_part, upper_part], axis=1).reshape(
        padded.shape[0], 2 * extent, 128
    )


def group_width(block_total):
    for stride in (16, 8, 4, 2):
        if block_total % stride == 0:
            return stride
    return 1


def bin_blocks(holding, weights, tile_count):
    row_count, block_count, lane_count = holding.shape
    field_count = row_count - 2
    stride = group_width(block_count) * lane_count
    weighted = (holding[:field_count] * weights[None]).reshape(
        field_count, block_count * lane_count
    )
    cell_row = holding[row_count - 1].reshape(block_count * lane_count)
    tile_values = jnp.arange(tile_count, dtype=jnp.float32)

    def add_group(counter, running):
        offset = counter * stride
        portion = lax.dynamic_slice_in_dim(weighted, offset, stride, 1)
        cell_slice = lax.dynamic_slice_in_dim(cell_row, offset, stride, 0)
        one_hot = (cell_slice[:, None] == tile_values[None, :]).astype(jnp.float32)
        return running + jnp.dot(
            portion, one_hot, precision=lax.Precision.HIGHEST, preferred_element_type=jnp.float32
        )

    return lax.fori_loop(
        0,
        block_count * lane_count // stride,
        add_group,
        jnp.zeros((field_count, tile_count), jnp.float32),
    )


def per_device(particle_fields, step_length, live_mask, dest_cell, block_counts, block_lists):
    field_count = particle_fields.shape[0]
    row_count = field_count + 2
    advanced = particle_fields[0:3] + step_length[None, :] * particle_fields[3:6]
    carried = jnp.concatenate(
        [
            advanced,
            particle_fields[3:],
            live_mask.astype(jnp.float32)[None, :],
            dest_cell.astype(jnp.float32)[None, :],
        ],
        axis=0,
    )
    blocks_held = carried.reshape(row_count, -1, 128)
    number = block_counts[0]
    entries = block_lists[0]
    first_end = 2 * CAP_X
    second_end = first_end + 2 * CAP_Z
    outgoing = pick_blocks(blocks_held, entries[:first_end], number[0], number[1])
    padded = padded_2(outgoing.reshape(row_count, -1), (("gx", 1),), CAP_X * 128)
    blocks_held = jnp.concatenate([blocks_held, arrived(padded, CAP_X)], axis=1)
    outgoing = pick_blocks(blocks_held, entries[first_end:second_end], number[2], number[3])
    padded = padded_2(outgoing.reshape(row_count, -1), (("gz", 1),), CAP_Z * 128)
    blocks_held = jnp.concatenate([blocks_held, arrived(padded, CAP_Z)], axis=1)
    outgoing = pick_blocks(blocks_held, entries[second_end:], number[4], number[5])
    block_index = jnp.arange(blocks_held.shape[1])
    limits = []
    for section_index, extent in enumerate((CAP_X, CAP_Z, CAP_Y)):
        for side_index in range(2):
            limits.append(jnp.broadcast_to(number[2 * section_index + side_index], (extent,)))
    wanted = jnp.concatenate(limits)
    position = jnp.concatenate(
        [jnp.arange(extent) for extent in (CAP_X, CAP_X, CAP_Z, CAP_Z, CAP_Y, CAP_Y)]
    )
    listed = (entries[:, None] == block_index[None, :]) & (position < wanted)[:, None]
    keep_block = 1.0 - jnp.any(listed, axis=0).astype(jnp.float32)
    weights = blocks_held[field_count] * keep_block[:, None]
    padded = padded_2(outgoing.reshape(row_count, -1), (("gy", 1),), CAP_Y * 128)
    landed = arrived(padded, CAP_Y)
    tile_sums = bin_blocks(blocks_held, weights, CELLS) + bin_blocks(
        landed, landed[field_count], CELLS
    )
    return tile_sums


def solution(mesh):
    placed = (
        P(None, ("gx", "gy", "gz")),
        P(("gx", "gy", "gz")),
        P(("gx", "gy", "gz")),
        P(("gx", "gy", "gz")),
        P(("gx", "gy", "gz"), None),
        P(("gx", "gy", "gz"), None),
    )
    return jax.shard_map(
        per_device,
        mesh=mesh,
        in_specs=placed,
        out_specs=P(None, ("gx", "gy", "gz")),
        check_vma=False,
    )
```

profile of v0, /device:TPU:0, one launch (start us, length us, event | category | flops | bytes accessed | tf_op | source)
XLA Modules:
  0.0 44.3 jit_solution(10634139163812123180)
XLA Ops:
  0.0 0.8 %fusion.17 = (s32[12]{0:T(128)S(1)}, s32[12]{0:T(128)S(1)}) fusion(s32[1,48]{1,0:T(1,128)} %param.15), kind=kLoop, calls=%fused_computation.61 | loop fusion | flops 72 | bytes 192 | tf_op jit(solution)/shard_map/jit(_take)/jit(_where)/select_n | solution.py:27
  0.8 0.8 %compare_and_fusion.1 = (pred[12]{0:T(512)(128)(4,1)S(1)}, pred[12]{0:T(512)(128)(4,1)S(1)}) fusion(s32[1,48]{1,0:T(1,128)} %param.15), kind=kLoop, calls=%fused_computation.54 | loop fusion | flops 144 | bytes 120 | tf_op jit(solution)/shard_map/jit(_take)/and | solution.py:27
  1.6 1.5 %fusion.24 = (s32[1,1]{1,0:T(1,128)}, s32[1,1]{1,0:T(1,128)}, s32[1,1]{1,0:T(1,128)}, s32[1,1]{1,0:T(1,128)}, s32[1,1]{1,0:T(1,128)}, /*index=5*/s32[1,1]{1,0:T(1,128)}) fusion(s32[1,6]{1,0:T(1,128)} %param.14), kind=kLoop, calls=%fused_computation.69 | loop fusion | bytes 48 | tf_op jit(solution)/shard_map/slice | solution.py:106
  3.2 1.3 %compare_convert_fusion.2 = f32[12]{0:T(128)S(1)} fusion(s32[]{:T(128)} %bitcast.9, s32[]{:T(128)} %bitcast.8), kind=kLoop, calls=%fused_computation.55 | loop fusion | flops 120 | bytes 56 | tf_op jit(solution)/shard_map/convert_element_type | solution.py:30
  4.5 1.2 %slice.104 = f32[17,8192]{1,0:T(8,128)S(1)} slice(f32[20,8192]{1,0:T(8,128)} %param.10), slice={[3:20], [0:8192]} | slice | bytes 1114112 | tf_op jit(solution)/shard_map/slice | solution.py:84
  5.9 0.3 copy.20
  6.3 0.3 copy-done.2
  6.6 1.1 %add_bitcast_fusion = f32[3,64,128]{2,0,1:T(4,128)S(1)} fusion(f32[20,8192]{1,0:T(8,128)} %param.10, f32[8192]{0:T(1024)S(1)} %copy-done.2), kind=kLoop, calls=%fused_computation.27 | loop fusion | flops 49152 | bytes 327680 | tf_op jit(solution)/shard_map/concatenate | solution.py:81
  7.9 0.6 %gather_fusion = f32[12,22,128]{2,1,0:T(8,128)S(1)} fusion(f32[22,64,128]{2,0,1:T(8,128)S(1)} %pad_maximum_fusion.2, s32[1024]{0:T(1024)S(1)} %get-tuple-element.266), kind=kCustom, calls=%fused_computation | custom fusion | bytes 270384 | tf_op jit(solution)/shard_map/jit(_take)/gather | solution.py:27
  8.7 0.5 %collective-permute-start = (f32[22,768]{1,0:T(8,128)S(1)}, f32[22,768]{1,0:T(8,128)S(1)}, u32[]{:S(2)}, u32[]{:S(2)}) collective-permute-start(f32[22,768]{1,0:T(8,128)S(1)} %get-tuple-element.253), channel_id=1, source_target_pairs={{0,8},{8,16},{16,24},{24,0},{1,9},{9,17},{17,25},{25,1},{2,10},{10... | collective-permute-start | bytes 202760 | tf_op jit(solution)/shard_map/ppermute | solution.py:19
  9.3 2.0 %collective-permute-start.1 = (f32[22,768]{1,0:T(8,128)S(1)}, f32[22,768]{1,0:T(8,128)S(1)}, u32[]{:S(2)}, u32[]{:S(2)}) collective-permute-start(f32[22,768]{1,0:T(8,128)S(1)} %get-tuple-element.254), channel_id=1, source_target_pairs={{8,0},{16,8},{24,16},{0,24},{9,1},{17,9},{25,17},{1,25},{10,2},{18... | collective-permute-start | bytes 202760 | tf_op jit(solution)/shard_map/ppermute | solution.py:20
  11.4 1.3 %compare_convert_fusion.1 = f32[12]{0:T(128)S(1)} fusion(s32[]{:T(128)} %bitcast.17, s32[]{:T(128)} %bitcast.16), kind=kLoop, calls=%fused_computation.53 | loop fusion | flops 120 | bytes 56 | tf_op jit(solution)/shard_map/convert_element_type | solution.py:30
  12.7 1.3 %compare_convert_fusion = f32[24]{0:T(128)S(1)} fusion(s32[]{:T(128)} %bitcast.21, s32[]{:T(128)} %bitcast.20), kind=kLoop, calls=%fused_computation.49 | loop fusion | flops 240 | bytes 104 | tf_op jit(solution)/shard_map/convert_element_type | solution.py:30
  14.3 0.6 %broadcast_in_dim.113 = s32[6]{0:T(128)S(1)} broadcast(s32[]{:T(128)} %bitcast.8), dimensions={} | broadcast | bytes 28 | tf_op jit(solution)/shard_map/broadcast_in_dim | solution.py:106
  14.9 0.6 %broadcast_in_dim.114 = s32[6]{0:T(128)S(1)} broadcast(s32[]{:T(128)} %bitcast.9), dimensions={} | broadcast | bytes 28 | tf_op jit(solution)/shard_map/broadcast_in_dim | solution.py:106
  15.5 0.6 %broadcast_in_dim.115 = s32[6]{0:T(128)S(1)} broadcast(s32[]{:T(128)} %bitcast.16), dimensions={} | broadcast | bytes 28 | tf_op jit(solution)/shard_map/broadcast_in_dim | solution.py:106
  16.1 0.7 %broadcast_in_dim.116 = s32[6]{0:T(128)S(1)} broadcast(s32[]{:T(128)} %bitcast.17), dimensions={} | broadcast | bytes 28 | tf_op jit(solution)/shard_map/broadcast_in_dim | solution.py:106
  16.8 0.6 %broadcast_in_dim.117 = s32[12]{0:T(128)S(1)} broadcast(s32[]{:T(128)} %bitcast.20), dimensions={} | broadcast | bytes 52 | tf_op jit(solution)/shard_map/broadcast_in_dim | solution.py:106
  17.4 0.6 %broadcast_in_dim.118 = s32[12]{0:T(128)S(1)} broadcast(s32[]{:T(128)} %bitcast.21), dimensions={} | broadcast | bytes 52 | tf_op jit(solution)/shard_map/broadcast_in_dim | solution.py:106
  18.4 0.2 pad_maximum_fusion.1
  18.6 0.6 %gather_fusion.1 = f32[12,22,128]{2,1,0:T(8,128)S(1)} fusion(f32[22,76,128]{2,0,1:T(8,128)S(1)} %pad_maximum_fusion.1, s32[1024]{0:T(1024)S(1)} %get-tuple-element.265), kind=kCustom, calls=%fused_computation.1 | custom fusion | bytes 270384 | tf_op jit(solution)/shard_map/jit(_take)/gather | solution.py:27
  19.3 2.3 %collective-permute-start.2 = (f32[22,768]{1,0:T(8,128)S(1)}, f32[22,768]{1,0:T(8,128)S(1)}, u32[]{:S(2)}, u32[]{:S(2)}) collective-permute-start(f32[22,768]{1,0:T(8,128)S(1)} %get-tuple-element.251), channel_id=1, source_target_pairs={{0,1},{1,0},{2,3},{3,2},{4,5},{5,4},{6,7},{7,6},{8,9},{9,8},{10,11... | collective-permute-start | bytes 202760 | tf_op jit(solution)/shard_map/ppermute | solution.py:19
  21.8 2.8 %collective-permute-done.2 = f32[22,768]{1,0:T(8,128)S(1)} collective-permute-done((f32[22,768]{1,0:T(8,128)S(1)}, f32[22,768]{1,0:T(8,128)S(1)}, u32[]{:S(2)}, u32[]{:S(2)}) %collective-permute-start.2) | collective-permute-done | bytes 67616 | tf_op jit(solution)/shard_map/ppermute | solution.py:19
  24.5 1.5 %collective-permute-done.3 = f32[22,768]{1,0:T(8,128)S(1)} collective-permute-done((f32[22,768]{1,0:T(8,128)S(1)}, f32[22,768]{1,0:T(8,128)S(1)}, u32[]{:S(2)}, u32[]{:S(2)}) %collective-permute-start.3) | collective-permute-done | bytes 67616 | tf_op jit(solution)/shard_map/ppermute | solution.py:20
  26.1 0.2 pad_maximum_fusion
  26.3 0.6 %gather_fusion.2 = f32[24,22,128]{2,1,0:T(8,128)S(1)} fusion(f32[22,88,128]{2,0,1:T(8,128)S(1)} %pad_maximum_fusion, s32[1024]{0:T(1024)S(1)} %pad_clamp_fusion), kind=kCustom, calls=%fused_computation.2 | custom fusion | bytes 540768 | tf_op jit(solution)/shard_map/jit(_take)/gather | solution.py:27
  27.1 1.7 %collective-permute-start.4 = (f32[22,1536]{1,0:T(8,128)S(1)}, f32[22,1536]{1,0:T(8,128)S(1)}, u32[]{:S(2)}, u32[]{:S(2)}) collective-permute-start(f32[22,1536]{1,0:T(8,128)S(1)} %get-tuple-element.250), channel_id=1, source_target_pairs={{0,2},{2,4},{4,6},{6,0},{1,3},{3,5},{5,7},{7,1},{8,10},{10,12},{12... | collective-permute-start | bytes 405512 | tf_op jit(solution)/shard_map/ppermute | solution.py:19
  28.8 2.2 %collective-permute-start.5 = (f32[22,1536]{1,0:T(8,128)S(1)}, f32[22,1536]{1,0:T(8,128)S(1)}, u32[]{:S(2)}, u32[]{:S(2)}) collective-permute-start(f32[22,1536]{1,0:T(8,128)S(1)} %get-tuple-element.249), channel_id=1, source_target_pairs={{2,0},{4,2},{6,4},{0,6},{3,1},{5,3},{7,5},{1,7},{10,8},{12,10},{14... | collective-permute-start | bytes 405512 | tf_op jit(solution)/shard_map/ppermute | solution.py:20
  31.0 0.2 fusion.19
  31.3 0.2 copy.26
  31.6 0.2 copy.31
  31.8 9.3 %while.28 = (s32[]{:T(128)}, f32[20,512]{1,0:T(8,128)S(1)}, f32[20,11264]{1,0:T(8,128)S(1)}, f32[11264]{0:T(1024)S(1)}, s32[]{:T(128)}, /*index=5*/s32[]{:T(128)}, s32[]{:T(128)}, s32[]{:T(128)}) while((s32[]{:T(128)}, f32[20,512]{1,0:T(8,128)S(1)}, f32[20,11264]{1,0:T(8,128)S(1)}, f32[11264]{0:T(1024)S(1)}, s32[]{:T(128)}, ...), condition=%wide.region_2.3_spmd.clone, body=%wide.region_1.2_spmd.clone.sunk | while | flops 126373896 | bytes 200853 | solution.py:69
  31.8 0.8 %fusion.30 = f32[20,512]{1,0:T(8,128)S(1)} fusion(f32[1024]{0:T(1024)S(1)} %dynamic_slice.41, f32[20,11264]{1,0:T(8,128)S(1)} %get-tuple-element.337, s32[]{:T(128)S(6)} %select_n.185, f32[20,512]{1,0:T(8,128)S(1)} %get-tuple-element.328, pred[]{:T(512)S(6)} %compare.6), kind=kOutput, calls=%fused_computation.7.clone.1 | convolution fusion | flops 126373888 | bytes 192517 | tf_op jit(solution)/shard_map/while/body/eval_jaxpr/dot_general | solution.py:65
  32.6 0.8 %fusion.30 = f32[20,512]{1,0:T(8,128)S(1)} fusion(f32[1024]{0:T(1024)S(1)} %dynamic_slice.41, f32[20,11264]{1,0:T(8,128)S(1)} %get-tuple-element.337, s32[]{:T(128)S(6)} %select_n.185, f32[20,512]{1,0:T(8,128)S(1)} %get-tuple-element.328, pred[]{:T(512)S(6)} %compare.6), kind=kOutput, calls=%fused_computation.7.clone.1 | convolution fusion | flops 126373888 | bytes 192517 | tf_op jit(solution)/shard_map/while/body/eval_jaxpr/dot_general | solution.py:65
  33.5 0.8 %fusion.30 = f32[20,512]{1,0:T(8,128)S(1)} fusion(f32[1024]{0:T(1024)S(1)} %dynamic_slice.41, f32[20,11264]{1,0:T(8,128)S(1)} %get-tuple-element.337, s32[]{:T(128)S(6)} %select_n.185, f32[20,512]{1,0:T(8,128)S(1)} %get-tuple-element.328, pred[]{:T(512)S(6)} %compare.6), kind=kOutput, calls=%fused_computation.7.clone.1 | convolution fusion | flops 126373888 | bytes 192517 | tf_op jit(solution)/shard_map/while/body/eval_jaxpr/dot_general | solution.py:65
  34.3 0.8 %fusion.30 = f32[20,512]{1,0:T(8,128)S(1)} fusion(f32[1024]{0:T(1024)S(1)} %dynamic_slice.41, f32[20,11264]{1,0:T(8,128)S(1)} %get-tuple-element.337, s32[]{:T(128)S(6)} %select_n.185, f32[20,512]{1,0:T(8,128)S(1)} %get-tuple-element.328, pred[]{:T(512)S(6)} %compare.6), kind=kOutput, calls=%fused_computation.7.clone.1 | convolution fusion | flops 126373888 | bytes 192517 | tf_op jit(solution)/shard_map/while/body/eval_jaxpr/dot_general | solution.py:65
  35.2 0.8 %fusion.30 = f32[20,512]{1,0:T(8,128)S(1)} fusion(f32[1024]{0:T(1024)S(1)} %dynamic_slice.41, f32[20,11264]{1,0:T(8,128)S(1)} %get-tuple-element.337, s32[]{:T(128)S(6)} %select_n.185, f32[20,512]{1,0:T(8,128)S(1)} %get-tuple-element.328, pred[]{:T(512)S(6)} %compare.6), kind=kOutput, calls=%fused_computation.7.clone.1 | convolution fusion | flops 126373888 | bytes 192517 | tf_op jit(solution)/shard_map/while/body/eval_jaxpr/dot_general | solution.py:65
  36.0 0.8 %fusion.30 = f32[20,512]{1,0:T(8,128)S(1)} fusion(f32[1024]{0:T(1024)S(1)} %dynamic_slice.41, f32[20,11264]{1,0:T(8,128)S(1)} %get-tuple-element.337, s32[]{:T(128)S(6)} %select_n.185, f32[20,512]{1,0:T(8,128)S(1)} %get-tuple-element.328, pred[]{:T(512)S(6)} %compare.6), kind=kOutput, calls=%fused_computation.7.clone.1 | convolution fusion | flops 126373888 | bytes 192517 | tf_op jit(solution)/shard_map/while/body/eval_jaxpr/dot_general | solution.py:65
  36.8 0.8 %fusion.30 = f32[20,512]{1,0:T(8,128)S(1)} fusion(f32[1024]{0:T(1024)S(1)} %dynamic_slice.41, f32[20,11264]{1,0:T(8,128)S(1)} %get-tuple-element.337, s32[]{:T(128)S(6)} %select_n.185, f32[20,512]{1,0:T(8,128)S(1)} %get-tuple-element.328, pred[]{:T(512)S(6)} %compare.6), kind=kOutput, calls=%fused_computation.7.clone.1 | convolution fusion | flops 126373888 | bytes 192517 | tf_op jit(solution)/shard_map/while/body/eval_jaxpr/dot_general | solution.py:65
  37.7 0.8 %fusion.30 = f32[20,512]{1,0:T(8,128)S(1)} fusion(f32[1024]{0:T(1024)S(1)} %dynamic_slice.41, f32[20,11264]{1,0:T(8,128)S(1)} %get-tuple-element.337, s32[]{:T(128)S(6)} %select_n.185, f32[20,512]{1,0:T(8,128)S(1)} %get-tuple-element.328, pred[]{:T(512)S(6)} %compare.6), kind=kOutput, calls=%fused_computation.7.clone.1 | convolution fusion | flops 126373888 | bytes 192517 | tf_op jit(solution)/shard_map/while/body/eval_jaxpr/dot_general | solution.py:65
  38.5 0.8 %fusion.30 = f32[20,512]{1,0:T(8,128)S(1)} fusion(f32[1024]{0:T(1024)S(1)} %dynamic_slice.41, f32[20,11264]{1,0:T(8,128)S(1)} %get-tuple-element.337, s32[]{:T(128)S(6)} %select_n.185, f32[20,512]{1,0:T(8,128)S(1)} %get-tuple-element.328, pred[]{:T(512)S(6)} %compare.6), kind=kOutput, calls=%fused_computation.7.clone.1 | convolution fusion | flops 126373888 | bytes 192517 | tf_op jit(solution)/shard_map/while/body/eval_jaxpr/dot_general | solution.py:65
  39.4 0.8 %fusion.30 = f32[20,512]{1,0:T(8,128)S(1)} fusion(f32[1024]{0:T(1024)S(1)} %dynamic_slice.41, f32[20,11264]{1,0:T(8,128)S(1)} %get-tuple-element.337, s32[]{:T(128)S(6)} %select_n.185, f32[20,512]{1,0:T(8,128)S(1)} %get-tuple-element.328, pred[]{:T(512)S(6)} %compare.6), kind=kOutput, calls=%fused_computation.7.clone.1 | convolution fusion | flops 126373888 | bytes 192517 | tf_op jit(solution)/shard_map/while/body/eval_jaxpr/dot_general | solution.py:65
  40.2 0.8 %fusion.30 = f32[20,512]{1,0:T(8,128)S(1)} fusion(f32[1024]{0:T(1024)S(1)} %dynamic_slice.41, f32[20,11264]{1,0:T(8,128)S(1)} %get-tuple-element.337, s32[]{:T(128)S(6)} %select_n.185, f32[20,512]{1,0:T(8,128)S(1)} %get-tuple-element.328, pred[]{:T(512)S(6)} %compare.6), kind=kOutput, calls=%fused_computation.7.clone.1 | convolution fusion | flops 126373888 | bytes 192517 | tf_op jit(solution)/shard_map/while/body/eval_jaxpr/dot_general | solution.py:65
  41.1 2.5 %while.29 = (s32[]{:T(128)}, f32[20,512]{1,0:T(8,128)S(1)}, f32[20,3072]{1,0:T(8,128)S(1)}, f32[3072]{0:T(1024)S(1)}, s32[]{:T(128)}, /*index=5*/s32[]{:T(128)}, s32[]{:T(128)}, s32[]{:T(128)}) while((s32[]{:T(128)}, f32[20,512]{1,0:T(8,128)S(1)}, f32[20,3072]{1,0:T(8,128)S(1)}, f32[3072]{0:T(1024)S(1)}, s32[]{:T(128)}, ...), condition=%wide.region_4.5_spmd.clone, body=%wide.region_3.4_spmd.clone.sunk | while | flops 126373896 | bytes 200853 | solution.py:69
  41.2 0.8 %fusion.32 = f32[20,512]{1,0:T(8,128)S(1)} fusion(f32[1024]{0:T(1024)S(1)} %dynamic_slice.43, f32[20,3072]{1,0:T(8,128)S(1)} %get-tuple-element.361, s32[]{:T(128)S(6)} %select_n.186, f32[20,512]{1,0:T(8,128)S(1)} %get-tuple-element.352, pred[]{:T(512)S(6)} %compare.7), kind=kOutput, calls=%fused_computation.13.clone.1 | convolution fusion | flops 126373888 | bytes 192517 | tf_op jit(solution)/shard_map/while/body/eval_jaxpr/dot_general | solution.py:65
  42.0 0.8 %fusion.32 = f32[20,512]{1,0:T(8,128)S(1)} fusion(f32[1024]{0:T(1024)S(1)} %dynamic_slice.43, f32[20,3072]{1,0:T(8,128)S(1)} %get-tuple-element.361, s32[]{:T(128)S(6)} %select_n.186, f32[20,512]{1,0:T(8,128)S(1)} %get-tuple-element.352, pred[]{:T(512)S(6)} %compare.7), kind=kOutput, calls=%fused_computation.13.clone.1 | convolution fusion | flops 126373888 | bytes 192517 | tf_op jit(solution)/shard_map/while/body/eval_jaxpr/dot_general | solution.py:65
  42.9 0.8 %fusion.32 = f32[20,512]{1,0:T(8,128)S(1)} fusion(f32[1024]{0:T(1024)S(1)} %dynamic_slice.43, f32[20,3072]{1,0:T(8,128)S(1)} %get-tuple-element.361, s32[]{:T(128)S(6)} %select_n.186, f32[20,512]{1,0:T(8,128)S(1)} %get-tuple-element.352, pred[]{:T(512)S(6)} %compare.7), kind=kOutput, calls=%fused_computation.13.clone.1 | convolution fusion | flops 126373888 | bytes 192517 | tf_op jit(solution)/shard_map/while/body/eval_jaxpr/dot_general | solution.py:65
  43.7 0.6 %add.149 = f32[20,512]{1,0:T(8,128)} add(f32[20,512]{1,0:T(8,128)S(1)} %get-tuple-element.193, f32[20,512]{1,0:T(8,128)S(1)} %get-tuple-element.194) | non-fusion elementwise | flops 10240 | bytes 122880 | tf_op jit(solution)/shard_map/add | solution.py:116
  (76 shorter events, 2.3 us)
Async XLA Ops:
  5.8 0.8 %copy-start.2 = (f32[8192]{0:T(1024)S(1)}, f32[8192]{0:T(1024)}, u32[]{:S(2)}) copy-start(f32[8192]{0:T(1024)} %param.11) | copy-start | bytes 98308
  5.9 1.8 %copy-start = (s32[8192]{0:T(1024)S(1)}, s32[8192]{0:T(1024)}, u32[]{:S(2)}) copy-start(s32[8192]{0:T(1024)} %param.12) | copy-start | bytes 98308
  5.9 1.8 %copy-start.1 = (s32[8192]{0:T(1024)S(1)}, s32[8192]{0:T(1024)}, u32[]{:S(2)}) copy-start(s32[8192]{0:T(1024)} %param.13) | copy-start | bytes 98308
  7.9 3.3 %copy-start.3 = (s32[1,48]{1,0:T(1,128)S(1)}, s32[1,48]{1,0:T(1,128)}, u32[]{:S(2)}) copy-start(s32[1,48]{1,0:T(1,128)} %param.15) | copy-start | bytes 580
  8.7 9.6 %collective-permute-start = (f32[22,768]{1,0:T(8,128)S(1)}, f32[22,768]{1,0:T(8,128)S(1)}, u32[]{:S(2)}, u32[]{:S(2)}) collective-permute-start(f32[22,768]{1,0:T(8,128)S(1)} %get-tuple-element.253), channel_id=1, source_target_pairs={{0,8},{8,16},{16,24},{24,0},{1,9},{9,17},{17,25},{25,1},{2,10},{10... | collective-permute-start | bytes 202760 | tf_op jit(solution)/shard_map/ppermute | solution.py:19
  9.3 9.0 %collective-permute-start.1 = (f32[22,768]{1,0:T(8,128)S(1)}, f32[22,768]{1,0:T(8,128)S(1)}, u32[]{:S(2)}, u32[]{:S(2)}) collective-permute-start(f32[22,768]{1,0:T(8,128)S(1)} %get-tuple-element.254), channel_id=1, source_target_pairs={{8,0},{16,8},{24,16},{0,24},{9,1},{17,9},{25,17},{1,25},{10,2},{18... | collective-permute-start | bytes 202760 | tf_op jit(solution)/shard_map/ppermute | solution.py:20
  19.3 5.2 %collective-permute-start.2 = (f32[22,768]{1,0:T(8,128)S(1)}, f32[22,768]{1,0:T(8,128)S(1)}, u32[]{:S(2)}, u32[]{:S(2)}) collective-permute-start(f32[22,768]{1,0:T(8,128)S(1)} %get-tuple-element.251), channel_id=1, source_target_pairs={{0,1},{1,0},{2,3},{3,2},{4,5},{5,4},{6,7},{7,6},{8,9},{9,8},{10,11... | collective-permute-start | bytes 202760 | tf_op jit(solution)/shard_map/ppermute | solution.py:19
  21.7 4.4 %collective-permute-start.3 = (f32[22,768]{1,0:T(8,128)S(1)}, f32[22,768]{1,0:T(8,128)S(1)}, u32[]{:S(2)}, u32[]{:S(2)}) collective-permute-start(f32[22,768]{1,0:T(8,128)S(1)} %get-tuple-element.252), channel_id=1, source_target_pairs={{1,0},{0,1},{3,2},{2,3},{5,4},{4,5},{7,6},{6,7},{9,8},{8,9},{11,10... | collective-permute-start | bytes 202760 | tf_op jit(solution)/shard_map/ppermute | solution.py:20
  27.1 13.9 %collective-permute-start.4 = (f32[22,1536]{1,0:T(8,128)S(1)}, f32[22,1536]{1,0:T(8,128)S(1)}, u32[]{:S(2)}, u32[]{:S(2)}) collective-permute-start(f32[22,1536]{1,0:T(8,128)S(1)} %get-tuple-element.250), channel_id=1, source_target_pairs={{0,2},{2,4},{4,6},{6,0},{1,3},{3,5},{5,7},{7,1},{8,10},{10,12},{12... | collective-permute-start | bytes 405512 | tf_op jit(solution)/shard_map/ppermute | solution.py:19
  28.8 12.2 %collective-permute-start.5 = (f32[22,1536]{1,0:T(8,128)S(1)}, f32[22,1536]{1,0:T(8,128)S(1)}, u32[]{:S(2)}, u32[]{:S(2)}) collective-permute-start(f32[22,1536]{1,0:T(8,128)S(1)} %get-tuple-element.249), channel_id=1, source_target_pairs={{2,0},{4,2},{6,4},{0,6},{3,1},{5,3},{7,5},{1,7},{10,8},{12,10},{14... | collective-permute-start | bytes 405512 | tf_op jit(solution)/shard_map/ppermute | solution.py:20
where the time goes:
time: 44.7 us; the launch traced here: 44.3 us
  matrix products  11.1 us (25%)
  local copies, waits for them, and re-layouts  10.7 us (24%)
  starting transfers between devices  8.81 us (20%)
  other arithmetic  8.32 us (19%)
  waiting for transfers between devices  4.28 us (10%)
  loops' own time  0.57 us (1%)
  between operations  0.5 us (1%)
    dot_general x14, matrix products, add_group(): jnp.dot(portion, one_hot, precision=lax.Precision.HIGHEST, preferred_elem...  11.1 us
    ppermute x3, starting transfers between devices, padded_2(): before = lax.ppermute(last, axis, up)  4.57 us
    ppermute x3, starting transfers between devices, padded_2(): after = lax.ppermute(initial, axis, down)  4.24 us
    convert_element_type x3, other arithmetic, pick_blocks(): usable = (position < wanted).astype(jnp.float32)  3.79 us
    broadcast_in_dim x6, local copies, waits for them, and re-layouts, per_device(): jnp.broadcast_to(number[2 * section_index + side_index], (extent,))  3.78 us
    ppermute x3, waiting for transfers between devices, padded_2(): before = lax.ppermute(last, axis, up)  2.77 us
    gather x6, local copies, waits for them, and re-layouts, pick_blocks(): picked = jnp.take(holding, chosen, axis=1)  1.81 us
    slice x1, local copies, waits for them, and re-layouts, per_device(): number[2 * section_index + side_index]  1.54 us
  transfers between devices with their start and end apart: 6, of which 2 were waited for; matrix products, arithmetic and copies ran while one was open for 37% of the time, Pallas kernels for 0%

commit v1 on v0

v1 whole, which is shorter than its diff:
```python
import jax
import jax.numpy as jnp
from jax import lax
from jax.experimental import pallas as pl
from jax.experimental.pallas import tpu as pltpu
from jax.sharding import PartitionSpec as P

CELLS = 512
CAP_X = 6
CAP_Z = 6
CAP_Y = 12
LANES = 128
SLAB = 24
GROUPS = CELLS // LANES
F32 = jnp.float32
BF16 = jnp.bfloat16

VMEM = pl.BlockSpec(memory_space=pltpu.VMEM)
SMEM = pl.BlockSpec(memory_space=pltpu.SMEM)


def params(mib):
    return pltpu.CompilerParams(vmem_limit_bytes=mib << 20)


def cost(flops, nbytes):
    return pl.CostEstimate(flops=flops, bytes_accessed=nbytes, transcendentals=0)


def pairwise(n):
    return n > 2 and n % 2 == 0


def flip_of(axis):
    return lax.axis_index(axis) % 2 if pairwise(lax.axis_size(axis)) else 0


def swapped_of(axis):
    return lax.axis_index(axis) % 2 if pairwise(lax.axis_size(axis)) else 1


def exchange(axis, bufs):
    n = lax.axis_size(axis)
    if n == 2:
        return [lax.ppermute(bufs[0], axis, [(0, 1), (1, 0)])]
    if pairwise(n):
        first = [(i, (i + 1) % n if i % 2 else (i - 1) % n) for i in range(n)]
        second = [(i, (i - 1) % n if i % 2 else (i + 1) % n) for i in range(n)]
    else:
        first = [(i, (i - 1) % n) for i in range(n)]
        second = [(i, (i + 1) % n) for i in range(n)]
    return [lax.ppermute(bufs[0], axis, first), lax.ppermute(bufs[1], axis, second)]


def buffer_shapes(axis, rows):
    n = lax.axis_size(axis)
    one = jax.ShapeDtypeStruct((2 * rows if n == 2 else rows, LANES), F32)
    return [one] if n == 2 else [one, one]


def half(refs, side, rows):
    if len(refs) == 1:
        return refs[0], side * rows
    return refs[side], 0


def packed_rows(fields, count):
    return -(-(count * (fields + 1)) // 8) * 8


def put_block(ref, base, slot, count, fields, slab):
    ref[pl.ds(base + slot * fields, fields), :] = slab[:fields]
    ref[pl.ds(base + count * fields + slot, 1), :] = slab[fields : fields + 1]


def get_block(ref, base, slot, count, fields):
    body = ref[pl.ds(base + slot * fields, fields), :]
    cell = ref[pl.ds(base + count * fields + slot, 1), :]
    pad = jnp.zeros((SLAB - fields - 1, LANES), F32)
    return jnp.concatenate([body, cell, pad], axis=0)


def drifted(fields_ref, step_ref, live_ref, cell_ref, block):
    lanes = pl.ds(pl.multiple_of(block * LANES, LANES), LANES)
    fields = fields_ref.shape[0]
    top = fields_ref[0:8, lanes]
    step = step_ref[pl.ds(block, 1), :]
    live = live_ref[pl.ds(block, 1), :].astype(F32)
    cell = cell_ref[pl.ds(block, 1), :].astype(F32)
    row = lax.broadcasted_iota(jnp.int32, (8, LANES), 0)
    top = top + jnp.where(row < 3, pltpu.roll(top, 5, 0) * step, 0.0)
    rest = fields_ref[8:fields, lanes]
    pad = jnp.zeros((SLAB - fields - 1, LANES), F32)
    return jnp.concatenate([top * live, rest * live, cell, pad], axis=0)


def binned(slabs):
    left, right = [], []
    lane_cell = lax.broadcasted_iota(jnp.int32, (LANES, LANES), 0)
    for slab, field in slabs:
        cell = slab[field : field + 1].astype(jnp.int32)
        low, group = cell & (LANES - 1), cell >> 7
        right.append(jnp.where(lane_cell == low, 1.0, 0.0).astype(BF16))
        high = slab.astype(BF16).astype(F32)
        both = jnp.concatenate([high, slab - high], axis=0)
        left.append(
            jnp.concatenate(
                [jnp.where(group == g, both, 0.0).astype(BF16) for g in range(GROUPS)], axis=0
            )
        )
    return lax.dot_general(
        jnp.concatenate(left, axis=1),
        jnp.concatenate(right, axis=1),
        (((1,), (1,)), ((), ())),
        preferred_element_type=F32,
    )


ACC = (GROUPS * 2 * SLAB, LANES)


def put_sums(ref, base, acc, fields):
    for g in range(GROUPS):
        top = 2 * SLAB * g
        ref[pl.ds(base + g * fields, fields), :] = (
            acc[top : top + fields] + acc[top + SLAB : top + SLAB + fields]
        )


def x_out_kernel(axis, fields, number, entries, f_ref, s_ref, l_ref, c_ref, *outs):
    flip = flip_of(axis)
    rows = packed_rows(fields, CAP_X)
    for side in range(2):
        way = flip if side == 0 else 1 - flip
        ref, base = half(outs, side, rows)
        for j in range(CAP_X):
            entry = entries[0, way * CAP_X + j]
            entry = jnp.where(j < number[0, way], entry, 0)
            slab = drifted(f_ref, s_ref, l_ref, c_ref, entry)
            put_block(ref, base, j, CAP_X, fields, slab * (j < number[0, way]).astype(F32))
        used = CAP_X * (fields + 1)
        if rows > used:
            ref[pl.ds(base + used, rows - used), :] = jnp.zeros((rows - used, LANES), F32)


def arrival_place(entry, first, cap, swapped):
    place = entry - first + cap * swapped
    return jnp.where(place >= 2 * cap, place - 2 * cap, place)


def pool_kernel(axes, fields, blocks, number, entries, f_ref, s_ref, l_ref, c_ref, pool, z_own, z_pick):
    x_axis, z_axis = axes

    @pl.loop(0, blocks, unroll=4)
    def _(b):
        pool[b] = drifted(f_ref, s_ref, l_ref, c_ref, b)

    flip = flip_of(z_axis)
    swapped = swapped_of(x_axis)
    for side in range(2):
        way = flip if side == 0 else 1 - flip
        for j in range(CAP_Z):
            slot = side * CAP_Z + j
            valid = j < number[0, 2 + way]
            entry = entries[0, 2 * CAP_X + way * CAP_Z + j]
            own = valid & (entry < blocks)
            z_own[slot] = pool[jnp.where(own, entry, 0)] * own.astype(F32)
            place = arrival_place(entry, blocks, CAP_X, swapped)
            place = jnp.where(valid & (entry >= blocks), place, -1)
            row = lax.broadcasted_iota(jnp.int32, (16, LANES), 0)
            z_pick[slot] = (row == place).astype(F32)


def make_z_out(fields, n_in):
    x_rows = packed_rows(fields, CAP_X)
    z_rows = packed_rows(fields, CAP_Z)

    def kernel(z_own, z_pick, *refs):
        arrivals, outs = refs[:n_in], refs[n_in:]
        came = []
        for place in range(2 * CAP_X):
            ref, base = half(arrivals, place // CAP_X, x_rows)
            came.append(get_block(ref, base, place % CAP_X, CAP_X, fields))
        for side in range(2):
            ref, base = half(outs, side, z_rows)
            for j in range(CAP_Z):
                slot = side * CAP_Z + j
                slab = z_own[slot]
                for place in range(2 * CAP_X):
                    slab = slab + came[place] * z_pick[slot, place : place + 1, :]
                put_block(ref, base, j, CAP_Z, fields, slab)
            used = CAP_Z * (fields + 1)
            if z_rows > used:
                ref[pl.ds(base + used, z_rows - used), :] = jnp.zeros((z_rows - used, LANES), F32)

    return kernel


def make_bin(fields, blocks, axes, n_in):
    x_axis, z_axis, y_axis = axes
    x_rows = packed_rows(fields, CAP_X)
    held = blocks + 2 * CAP_X
    total = held + 2 * CAP_Z

    def kernel(number, entries, pool, *refs):
        arrivals = refs[:n_in]
        stay, y_part, z_mask, codes, x_pool, y_acc = refs[n_in:]
        x_swapped, z_swapped, y_flip = swapped_of(x_axis), swapped_of(z_axis), flip_of(y_axis)
        for place in range(2 * CAP_X):
            ref, base = half(arrivals, place // CAP_X, x_rows)
            x_pool[place] = get_block(ref, base, place % CAP_X, CAP_X, fields)

        for b in range(total + 1):
            codes[b] = 0

        def spot(entry):
            in_x = arrival_place(entry, blocks, CAP_X, x_swapped) + blocks
            in_z = arrival_place(entry, held, CAP_Z, z_swapped) + held
            return jnp.where(entry < blocks, entry, jnp.where(entry < held, in_x, in_z))

        at = 0
        for section, cap in enumerate((CAP_X, CAP_Z, CAP_Y)):
            for way in range(2):
                for j in range(cap):
                    valid = j < number[0, 2 * section + way]
                    code = 1 if section < 2 else 2 + (way if isinstance(y_flip, int) else way ^ y_flip)
                    codes[jnp.where(valid, spot(entries[0, at]), total)] = code
                    at += 1

        for b in range(2 * CAP_Z):
            code = codes[held + b]
            for k in range(3):
                wanted = (0, 2, 3)[k]
                z_mask[k, b : b + 1, :] = jnp.full((1, LANES), (code == wanted).astype(F32))

        first = 2 * CAP_X + 2 * CAP_Z
        for side in range(2):
            way = side if isinstance(y_flip, int) else side ^ y_flip

            def one(j):
                entry = spot(entries[0, first + way * CAP_Y + j])
                valid = (j < number[0, 4 + way]) & (entry < held)
                own = valid & (entry < blocks)
                mine = pool[jnp.where(own, entry, 0)] * own.astype(F32)
                theirs = valid & (entry >= blocks)
                return mine + x_pool[jnp.where(theirs, entry - blocks, 0)] * theirs.astype(F32)

            acc = jnp.zeros(ACC, F32)
            for j in range(0, CAP_Y, 4):
                acc = acc + binned([(one(j + i), fields) for i in range(4)])
            y_part[side] = acc

        y_acc[...] = jnp.zeros(ACC, F32)

        @pl.loop(0, blocks // 8)
        def _(step):
            slabs = []
            for i in range(8):
                b = step * 8 + i
                slabs.append((keep_block(pool[b], codes[b] == 0, fields), fields))
            y_acc[...] += binned(slabs)

        acc = y_acc[...]
        for p in range(0, 2 * CAP_X, 6):
            slabs = []
            for i in range(6):
                slabs.append((keep_block(x_pool[p + i], codes[blocks + p + i] == 0, fields), fields))
            acc = acc + binned(slabs)
        stay[...] = acc

    return kernel


def keep_block(slab, keep, fields):
    row = lax.broadcasted_iota(jnp.int32, (SLAB, LANES), 0)
    return slab * jnp.where(row == fields, 1.0, keep.astype(F32))


def z_slab(arrivals, mask, kind, place, rows, fields):
    ref, base = half(arrivals, place // CAP_Z, rows)
    body = ref[pl.ds(base + (place % CAP_Z) * fields, fields), :] * mask[kind, place : place + 1, :]
    cell = ref[pl.ds(base + CAP_Z * fields + place % CAP_Z, 1), :]
    pad = jnp.zeros((SLAB - fields - 1, LANES), F32)
    return jnp.concatenate([body, cell, pad], axis=0)


def make_y_out(fields, n_in):
    rows = packed_rows(fields, CAP_Z)

    def kernel(y_part, z_mask, *refs):
        arrivals, outs = refs[:n_in], refs[n_in:]
        for side in range(2):
            slabs = [
                (z_slab(arrivals, z_mask, 1 + side, place, rows, fields), fields)
                for place in range(2 * CAP_Z)
            ]
            ref, base = half(outs, side, GROUPS * fields)
            put_sums(ref, base, y_part[side] + binned(slabs), fields)

    return kernel


def make_stay(fields, n_in):
    rows = packed_rows(fields, CAP_Z)

    def kernel(stay, z_mask, *refs):
        arrivals, out = refs[:n_in], refs[n_in]
        slabs = [
            (z_slab(arrivals, z_mask, 0, place, rows, fields), fields) for place in range(2 * CAP_Z)
        ]
        put_sums(out, 0, stay[...] + binned(slabs), fields)

    return kernel


def make_final(fields, n_in):
    def kernel(stay, *refs):
        arrivals, out = refs[:n_in], refs[n_in]
        for g in range(GROUPS):
            total = stay[g * fields : (g + 1) * fields, :]
            for side in range(2):
                ref, base = half(arrivals, side, GROUPS * fields)
                total = total + ref[pl.ds(base + g * fields, fields), :]
            out[:, g * LANES : (g + 1) * LANES] = total

    return kernel


def per_device(particle_fields, step_length, live_mask, dest_cell, block_counts, block_lists):
    fields = particle_fields.shape[0]
    blocks = particle_fields.shape[1] // LANES
    data = (
        particle_fields,
        step_length.reshape(blocks, LANES),
        live_mask.reshape(blocks, LANES),
        dest_cell.reshape(blocks, LANES),
    )
    lists = (block_counts, block_lists)

    def shape(*dims):
        return jax.ShapeDtypeStruct(dims, F32)

    x_rows, z_rows, y_rows = packed_rows(fields, CAP_X), packed_rows(fields, CAP_Z), GROUPS * fields
    x_bufs, z_bufs, y_bufs = (
        buffer_shapes("gx", x_rows),
        buffer_shapes("gz", z_rows),
        buffer_shapes("gy", y_rows),
    )

    def x_out(*refs):
        x_out_kernel("gx", fields, *refs)

    out = pl.pallas_call(
        x_out,
        out_shape=x_bufs,
        in_specs=[SMEM] * 2 + [VMEM] * 4,
        out_specs=[VMEM] * len(x_bufs),
        compiler_params=params(8),
        cost_estimate=cost(1 << 16, 1 << 20),
        name="x_out",
    )(*lists, *data)
    x_in = exchange("gx", out)

    def pool_body(*refs):
        pool_kernel(("gx", "gz"), fields, blocks, *refs)

    pool, z_own, z_pick = pl.pallas_call(
        pool_body,
        out_shape=[
            shape(blocks, SLAB, LANES),
            shape(2 * CAP_Z, SLAB, LANES),
            shape(2 * CAP_Z, 16, LANES),
        ],
        in_specs=[SMEM] * 2 + [VMEM] * 4,
        out_specs=[VMEM] * 3,
        compiler_params=params(8),
        cost_estimate=cost(1 << 22, 1 << 20),
        name="pool",
    )(*lists, *data)

    out = pl.pallas_call(
        make_z_out(fields, len(x_in)),
        out_shape=z_bufs,
        in_specs=[VMEM] * (2 + len(x_in)),
        out_specs=[VMEM] * len(z_bufs),
        compiler_params=params(8),
        cost_estimate=cost(1 << 16, 1 << 19),
        name="z_out",
    )(z_own, z_pick, *x_in)
    z_in = exchange("gz", out)

    stay, y_part, z_mask = pl.pallas_call(
        make_bin(fields, blocks, ("gx", "gz", "gy"), len(x_in)),
        out_shape=[shape(*ACC), shape(2, *ACC), shape(3, 16, LANES)],
        in_specs=[SMEM] * 2 + [VMEM] * (1 + len(x_in)),
        out_specs=[VMEM] * 3,
        scratch_shapes=[
            pltpu.SMEM((blocks + 2 * CAP_X + 2 * CAP_Z + 1,), jnp.int32),
            pltpu.VMEM((2 * CAP_X, SLAB, LANES), F32),
            pltpu.VMEM(ACC, F32),
        ],
        compiler_params=params(12),
        cost_estimate=cost(1 << 27, 1 << 20),
        name="bin_held",
    )(*lists, pool, *x_in)

    out = pl.pallas_call(
        make_y_out(fields, len(z_in)),
        out_shape=y_bufs,
        in_specs=[VMEM] * (2 + len(z_in)),
        out_specs=[VMEM] * len(y_bufs),
        compiler_params=params(8),
        cost_estimate=cost(1 << 20, 1 << 19),
        name="y_out",
    )(y_part, z_mask, *z_in)
    y_in = exchange("gy", out)

    stay = pl.pallas_call(
        make_stay(fields, len(z_in)),
        out_shape=shape(y_rows, LANES),
        in_specs=[VMEM] * (2 + len(z_in)),
        out_specs=VMEM,
        compiler_params=params(8),
        cost_estimate=cost(1 << 22, 1 << 19),
        name="bin_z",
    )(stay, z_mask, *z_in)

    return pl.pallas_call(
        make_final(fields, len(y_in)),
        out_shape=shape(fields, CELLS),
        in_specs=[VMEM] * (1 + len(y_in)),
        out_specs=VMEM,
        compiler_params=params(8),
        cost_estimate=cost(1 << 16, 1 << 17),
        name="final",
    )(stay, *y_in)


def solution(mesh):
    axes = ("gx", "gy", "gz")
    placed = (P(None, axes), P(axes), P(axes), P(axes), P(axes, None), P(axes, None))
    return jax.shard_map(
        per_device, mesh=mesh, in_specs=placed, out_specs=P(None, axes), check_vma=False
    )
```

time: 44.7 us -> 25.5 us (0.57)
  matrix products: 11.1 us -> 0 us
  other arithmetic: 8.32 us -> 0 us
  Pallas kernels: 0 us -> 7.03 us
  local copies, waits for them, and re-layouts: 10.7 us -> 4.07 us
  loops' own time: 0.57 us -> 0 us
  starting transfers between devices: 8.81 us -> 9.33 us
  between operations: 0.5 us -> 0.05 us
    dot_general x14 -> x0, matrix products: 11.1 us -> none  [add_group(): jnp.dot(portion, one_hot, precision=lax.Precision.HIGHEST, preferred_elem...]
    pallas_call x0 -> x7, Pallas kernels: none -> 7.03 us  [the longest x1 4 us: per_device(): pl.pallas_call(make_bin(fields, blocks, ('gx', 'gz', 'gy'), len(x_in)), o...]
    broadcast_in_dim x8 -> x0, local copies, waits for them, and re-layouts: 3.93 us -> none  [the longest x6 3.78 us: per_device(): jnp.broadcast_to(number[2 * section_index + side_index], (extent,))]
    convert_element_type x5 -> x0, other arithmetic: 3.8 us -> none  [the longest x3 3.79 us: pick_blocks(): usable = (position < wanted).astype(jnp.float32)]
    unnamed x18 -> x12, local copies, waits for them, and re-layouts: 0.97 us -> 4.07 us
    slice x6 -> x0, local copies, waits for them, and re-layouts: 2.8 us -> none  [the longest x1 1.54 us: per_device(): number[2 * section_index + side_index]]
    gather x6 -> x0, local copies, waits for them, and re-layouts: 1.81 us -> none  [pick_blocks(): picked = jnp.take(holding, chosen, axis=1)]
    concatenate x6 -> x0, other arithmetic: 1.62 us -> none  [the longest x2 1.25 us: per_device(): jnp.concatenate([advanced, particle_fields[3:], live_mask.astype(jnp.floa...]
  transfers between devices with their start and end apart: 6 -> 5, of which waited for: 2 -> 3; matrix products, arithmetic and copies ran while one was open for 37% -> 0% of each run, Pallas kernels for 0% -> 21%
where the time goes in v1:
time: 25.5 us; the launch traced here: 25.1 us
  starting transfers between devices  9.33 us (37%)
  Pallas kernels  7.03 us (28%)
  waiting for transfers between devices  4.63 us (18%)
  local copies, waits for them, and re-layouts  4.07 us (16%)
    ppermute x2, starting transfers between devices, exchange(): lax.ppermute(bufs[0], axis, first)  6.13 us
    unnamed x12, local copies, waits for them, and re-layouts  4.07 us
    pallas_call x1, Pallas kernels, per_device(): pl.pallas_call(make_bin(fields, blocks, ('gx', 'gz', 'gy'), len(x_in)), o...  4 us
    ppermute x2, waiting for transfers between devices, exchange(): lax.ppermute(bufs[0], axis, first)  2.83 us
    ppermute x1, starting transfers between devices, exchange(): return [lax.ppermute(bufs[0], axis, [(0, 1), (1, 0)])]  2.51 us
    ppermute x2, waiting for transfers between devices, exchange(): lax.ppermute(bufs[1], axis, second)  1.8 us
    pallas_call x1, Pallas kernels, per_device(): pl.pallas_call(pool_body, out_shape=[shape(blocks, SLAB, LANES), shape(2...  0.84 us
    ppermute x2, starting transfers between devices, exchange(): lax.ppermute(bufs[1], axis, second)  0.68 us
  transfers between devices with their start and end apart: 5, of which 3 were waited for; matrix products, arithmetic and copies ran while one was open for 0% of the time, Pallas kernels for 21%

profile of v1, /device:TPU:0, one launch (start us, length us, event | category | flops | bytes accessed | tf_op | source)
XLA Modules:
  0.0 25.1 jit_solution(11556073468534657595)
XLA Ops:
  0.0 0.0 copy-start.4
  0.0 0.0 copy-start.5
  0.0 0.7 %copy-done.4 = s32[1,6]{1,0:T(1,128)S(1)} copy-done((s32[1,6]{1,0:T(1,128)S(1)}, s32[1,6]{1,0:T(1,128)}, u32[]{:S(2)}) %copy-start.4) | copy-done | bytes 48
  0.7 0.0 copy-done.5
  0.7 0.0 copy-start
  0.7 1.1 %copy-done = f32[20,8192]{1,0:T(8,128)S(1)} copy-done((f32[20,8192]{1,0:T(8,128)S(1)}, f32[20,8192]{1,0:T(8,128)}, u32[]{:S(2)}) %copy-start) | copy-done | bytes 655384
  1.8 0.0 copy-start.1
  1.8 0.8 %copy-done.1 = f32[8192]{0:T(1024)S(1)} copy-done((f32[8192]{0:T(1024)S(1)}, f32[8192]{0:T(1024)}, u32[]{:S(2)}) %copy-start.1) | copy-done | bytes 32792
  2.6 0.0 copy-start.2
  2.6 0.8 %copy-done.2 = s32[8192]{0:T(1024)S(1)} copy-done((s32[8192]{0:T(1024)S(1)}, s32[8192]{0:T(1024)}, u32[]{:S(2)}) %copy-start.2) | copy-done | bytes 32792
  3.3 0.0 copy-start.3
  3.3 0.8 %copy-done.3 = s32[8192]{0:T(1024)S(1)} copy-done((s32[8192]{0:T(1024)S(1)}, s32[8192]{0:T(1024)}, u32[]{:S(2)}) %copy-start.3) | copy-done | bytes 32792
  4.1 0.6 %x_out.1 = (f32[128,128]{1,0:T(8,128)S(1)}, f32[128,128]{1,0:T(8,128)S(1)}) custom-call(s32[1,6]{1,0:T(1,128)S(1)} %copy-done.4, s32[1,48]{1,0:T(1,128)S(1)} %copy-done.5, f32[20,8192]{1,0:T(8,128)S(1)} %copy-done, f32[64,128]{1,0:T(8,128)S(1)} %bitcast.3, s32[64,128]{1,0:T(8,128)S(1)} %bitcast.5, s32[64,128]{1,0:T(8,128)S(1)} %bitcast.7), custom_call_target="tpu_custom_call" | custom-call | flops 65536 | bytes 1048576 | tf_op jit(solution)/shard_map/x_out/pallas_call | solution.py:353
  4.7 2.5 %collective-permute-start = (f32[128,128]{1,0:T(8,128)S(1)}, f32[128,128]{1,0:T(8,128)S(1)}, u32[]{:S(2)}, u32[]{:S(2)}) collective-permute-start(f32[128,128]{1,0:T(8,128)S(1)} %get-tuple-element.16), channel_id=1, source_target_pairs={{0,24},{8,16},{16,8},{24,0},{1,25},{9,17},{17,9},{25,1},{2,26},{10... | collective-permute-start | bytes 196616 | tf_op jit(solution)/shard_map/ppermute | solution.py:52
  7.2 0.7 %collective-permute-start.1 = (f32[128,128]{1,0:T(8,128)S(1)}, f32[128,128]{1,0:T(8,128)S(1)}, u32[]{:S(2)}, u32[]{:S(2)}) collective-permute-start(f32[128,128]{1,0:T(8,128)S(1)} %get-tuple-element.17), channel_id=1, source_target_pairs={{0,8},{8,0},{16,24},{24,16},{1,9},{9,1},{17,25},{25,17},{2,10},{10... | collective-permute-start | bytes 196616 | tf_op jit(solution)/shard_map/ppermute | solution.py:52
  7.9 0.8 %pool.1 = (f32[64,24,128]{2,1,0:T(8,128)S(1)}, f32[12,24,128]{2,1,0:T(8,128)S(1)}, f32[12,16,128]{2,1,0:T(8,128)S(1)}) custom-call(s32[1,6]{1,0:T(1,128)S(1)} %copy-done.4, s32[1,48]{1,0:T(1,128)S(1)} %copy-done.5, f32[20,8192]{1,0:T(8,128)S(1)} %copy-done, f32[64,128]{1,0:T(8,128)S(1)} %bitcast.4, s32[64,128]{1,0:T(8,128)S(1)} %bitcast.6, s32[64,128]{1,0:T(8,128)S(1)} %bitcast.8), custom_call_target="tpu_custom_call" | custom-call | flops 4194304 | bytes 1048576 | tf_op jit(solution)/shard_map/pool/pallas_call | solution.py:367
  8.7 1.0 %collective-permute-done.refs_0_ = f32[128,128]{1,0:T(8,128)S(1)} collective-permute-done((f32[128,128]{1,0:T(8,128)S(1)}, f32[128,128]{1,0:T(8,128)S(1)}, u32[]{:S(2)}, u32[]{:S(2)}) %collective-permute-start) | collective-permute-done | bytes 65568 | tf_op jit(solution)/shard_map/ppermute | solution.py:52
  9.7 0.0 collective-permute-done.1.refs_1_
  9.7 0.1 z_out.1
  9.8 2.5 %collective-permute-start.2 = (f32[256,128]{1,0:T(8,128)S(1)}, f32[256,128]{1,0:T(8,128)S(1)}, u32[]{:S(2)}, u32[]{:S(2)}) collective-permute-start(f32[256,128]{1,0:T(8,128)S(1)} %z_out.1), channel_id=1, source_target_pairs={{0,1},{1,0},{2,3},{3,2},{4,5},{5,4},{6,7},{7,6},{8,9},{9,8},{10,11... | collective-permute-start | bytes 393224 | tf_op jit(solution)/shard_map/ppermute | solution.py:45
  12.3 4.0 %bin_held.1 = (f32[192,128]{1,0:T(8,128)S(1)}, f32[2,192,128]{2,1,0:T(8,128)S(1)}, f32[3,16,128]{2,1,0:T(8,128)S(1)}) custom-call(s32[1,6]{1,0:T(1,128)S(1)} %copy-done.4, s32[1,48]{1,0:T(1,128)S(1)} %copy-done.5, f32[64,24,128]{2,1,0:T(8,128)S(1)} %get-tuple-element.15.pool, f32[128,128]{1,0:T(8,128)S(1)} %collective-permute-done.refs_0_, ...), custom_call_target="tpu_custom_call" | custom-call | flops 134217728 | bytes 1048576 | tf_op jit(solution)/shard_map/bin_held/pallas_call | solution.py:392
  16.3 0.0 collective-permute-done.2.refs_0_
  16.3 0.5 %y_out.1 = (f32[80,128]{1,0:T(8,128)S(1)}, f32[80,128]{1,0:T(8,128)S(1)}) custom-call(f32[2,192,128]{2,1,0:T(8,128)S(1)} %get-tuple-element.22.y_part, f32[3,16,128]{2,1,0:T(8,128)S(1)} %get-tuple-element.19.z_mask, f32[256,128]{1,0:T(8,128)S(1)} %collective-permute-done.2.refs_0_), custom_call_target="tpu_custom_call" | custom-call | flops 1048576 | bytes 524288 | tf_op jit(solution)/shard_map/y_out/pallas_call | solution.py:407
  16.8 3.7 %collective-permute-start.3 = (f32[80,128]{1,0:T(8,128)S(1)}, f32[80,128]{1,0:T(8,128)S(1)}, u32[]{:S(2)}, u32[]{:S(2)}) collective-permute-start(f32[80,128]{1,0:T(8,128)S(1)} %get-tuple-element.23), channel_id=1, source_target_pairs={{0,6},{2,4},{4,2},{6,0},{1,7},{3,5},{5,3},{7,1},{8,14},{10,12},{12... | collective-permute-start | bytes 122888 | tf_op jit(solution)/shard_map/ppermute | solution.py:52
  20.5 0.0 collective-permute-start.4
  20.5 0.3 %bin_z.1.stay = f32[80,128]{1,0:T(8,128)S(1)} custom-call(f32[192,128]{1,0:T(8,128)S(1)} %get-tuple-element.18.stay, f32[3,16,128]{2,1,0:T(8,128)S(1)} %get-tuple-element.19.z_mask, f32[256,128]{1,0:T(8,128)S(1)} %collective-permute-done.2.refs_0_), custom_call_target="tpu_custom_call" | custom-call | flops 4194304 | bytes 524288 | tf_op jit(solution)/shard_map/bin_z/pallas_call | solution.py:418
  20.8 1.9 %collective-permute-done.3.refs_0_ = f32[80,128]{1,0:T(8,128)S(1)} collective-permute-done((f32[80,128]{1,0:T(8,128)S(1)}, f32[80,128]{1,0:T(8,128)S(1)}, u32[]{:S(2)}, u32[]{:S(2)}) %collective-permute-start.3) | collective-permute-done | bytes 40992 | tf_op jit(solution)/shard_map/ppermute | solution.py:52
  22.7 1.8 %collective-permute-done.4.refs_1_ = f32[80,128]{1,0:T(8,128)S(1)} collective-permute-done((f32[80,128]{1,0:T(8,128)S(1)}, f32[80,128]{1,0:T(8,128)S(1)}, u32[]{:S(2)}, u32[]{:S(2)}) %collective-permute-start.4) | collective-permute-done | bytes 40992 | tf_op jit(solution)/shard_map/ppermute | solution.py:52
  24.5 0.6 %final.1 = f32[20,512]{1,0:T(8,128)} custom-call(f32[80,128]{1,0:T(8,128)S(1)} %bin_z.1.stay, f32[80,128]{1,0:T(8,128)S(1)} %collective-permute-done.3.refs_0_, f32[80,128]{1,0:T(8,128)S(1)} %collective-permute-done.4.refs_1_), custom_call_target="tpu_custom_call" | custom-call | flops 65536 | bytes 131072 | tf_op jit(solution)/shard_map/final/pallas_call | solution.py:428
Async XLA Ops:
  0.0 0.7 %copy-start.4 = (s32[1,6]{1,0:T(1,128)S(1)}, s32[1,6]{1,0:T(1,128)}, u32[]{:S(2)}) copy-start(s32[1,6]{1,0:T(1,128)} %number.1) | copy-start | bytes 76
  0.0 0.7 %copy-start.5 = (s32[1,48]{1,0:T(1,128)S(1)}, s32[1,48]{1,0:T(1,128)}, u32[]{:S(2)}) copy-start(s32[1,48]{1,0:T(1,128)} %entries.1) | copy-start | bytes 580
  0.7 1.1 %copy-start = (f32[20,8192]{1,0:T(8,128)S(1)}, f32[20,8192]{1,0:T(8,128)}, u32[]{:S(2)}) copy-start(f32[20,8192]{1,0:T(8,128)} %refs_2_.3) | copy-start | bytes 1966084
  1.8 0.8 %copy-start.1 = (f32[8192]{0:T(1024)S(1)}, f32[8192]{0:T(1024)}, u32[]{:S(2)}) copy-start(f32[8192]{0:T(1024)} %param.7) | copy-start | bytes 98308
  2.6 0.8 %copy-start.2 = (s32[8192]{0:T(1024)S(1)}, s32[8192]{0:T(1024)}, u32[]{:S(2)}) copy-start(s32[8192]{0:T(1024)} %param.8) | copy-start | bytes 98308
  3.3 0.8 %copy-start.3 = (s32[8192]{0:T(1024)S(1)}, s32[8192]{0:T(1024)}, u32[]{:S(2)}) copy-start(s32[8192]{0:T(1024)} %param.9) | copy-start | bytes 98308
  4.7 5.0 %collective-permute-start = (f32[128,128]{1,0:T(8,128)S(1)}, f32[128,128]{1,0:T(8,128)S(1)}, u32[]{:S(2)}, u32[]{:S(2)}) collective-permute-start(f32[128,128]{1,0:T(8,128)S(1)} %get-tuple-element.16), channel_id=1, source_target_pairs={{0,24},{8,16},{16,8},{24,0},{1,25},{9,17},{17,9},{25,1},{2,26},{10... | collective-permute-start | bytes 196616 | tf_op jit(solution)/shard_map/ppermute | solution.py:52
  7.2 2.5 %collective-permute-start.1 = (f32[128,128]{1,0:T(8,128)S(1)}, f32[128,128]{1,0:T(8,128)S(1)}, u32[]{:S(2)}, u32[]{:S(2)}) collective-permute-start(f32[128,128]{1,0:T(8,128)S(1)} %get-tuple-element.17), channel_id=1, source_target_pairs={{0,8},{8,0},{16,24},{24,16},{1,9},{9,1},{17,25},{25,17},{2,10},{10... | collective-permute-start | bytes 196616 | tf_op jit(solution)/shard_map/ppermute | solution.py:52
  9.8 6.5 %collective-permute-start.2 = (f32[256,128]{1,0:T(8,128)S(1)}, f32[256,128]{1,0:T(8,128)S(1)}, u32[]{:S(2)}, u32[]{:S(2)}) collective-permute-start(f32[256,128]{1,0:T(8,128)S(1)} %z_out.1), channel_id=1, source_target_pairs={{0,1},{1,0},{2,3},{3,2},{4,5},{5,4},{6,7},{7,6},{8,9},{9,8},{10,11... | collective-permute-start | bytes 393224 | tf_op jit(solution)/shard_map/ppermute | solution.py:45
  16.8 5.9 %collective-permute-start.3 = (f32[80,128]{1,0:T(8,128)S(1)}, f32[80,128]{1,0:T(8,128)S(1)}, u32[]{:S(2)}, u32[]{:S(2)}) collective-permute-start(f32[80,128]{1,0:T(8,128)S(1)} %get-tuple-element.23), channel_id=1, source_target_pairs={{0,6},{2,4},{4,2},{6,0},{1,7},{3,5},{5,3},{7,1},{8,14},{10,12},{12... | collective-permute-start | bytes 122888 | tf_op jit(solution)/shard_map/ppermute | solution.py:52
  20.5 4.0 %collective-permute-start.4 = (f32[80,128]{1,0:T(8,128)S(1)}, f32[80,128]{1,0:T(8,128)S(1)}, u32[]{:S(2)}, u32[]{:S(2)}) collective-permute-start(f32[80,128]{1,0:T(8,128)S(1)} %get-tuple-element.24), channel_id=1, source_target_pairs={{0,2},{2,0},{4,6},{6,4},{1,3},{3,1},{5,7},{7,5},{8,10},{10,8},{12,... | collective-permute-start | bytes 122888 | tf_op jit(solution)/shard_map/ppermute | solution.py:52

commit v2 on v1

--- a/solution.py
+++ b/solution.py
@@ -17,6 +17,8 @@
 
 VMEM = pl.BlockSpec(memory_space=pltpu.VMEM)
 SMEM = pl.BlockSpec(memory_space=pltpu.SMEM)
+HBM = pl.BlockSpec(memory_space=pltpu.HBM)
+CHUNKS = 4
 
 
 def params(mib):
@@ -127,7 +129,25 @@
         )
 
 
-def x_out_kernel(axis, fields, number, entries, f_ref, s_ref, l_ref, c_ref, *outs):
+def x_out_kernel(axis, number_hbm, entries_hbm, f_hbm, s_hbm, l_hbm, c_hbm, *refs):
+    outs, (f_ref, s_ref, l_ref, c_ref), (number, entries, sems) = refs[:-7], refs[-7:-3], refs[-3:]
+    fields, lanes = f_ref.shape
+    copies = [
+        pltpu.make_async_copy(src, dst, sems.at[i])
+        for i, (src, dst) in enumerate(
+            ((number_hbm, number), (entries_hbm, entries), (s_hbm, s_ref), (l_hbm, l_ref), (c_hbm, c_ref))
+        )
+    ]
+    part = lanes // CHUNKS
+    for i in range(CHUNKS):
+        cut = pl.ds(i * part, part)
+        copies.append(
+            pltpu.make_async_copy(f_hbm.at[:, cut], f_ref.at[:, cut], sems.at[5 + i])
+        )
+    for copy in copies:
+        copy.start()
+    for copy in copies:
+        copy.wait()
     flip = flip_of(axis)
     rows = packed_rows(fields, CAP_X)
     for side in range(2):
@@ -196,7 +216,7 @@
     return kernel
 
 
-def make_bin(fields, blocks, axes, n_in):
+def make_bin(fields, blocks, early, axes, n_in):
     x_axis, z_axis, y_axis = axes
     x_rows = packed_rows(fields, CAP_X)
     held = blocks + 2 * CAP_X
@@ -204,7 +224,7 @@
 
     def kernel(number, entries, pool, *refs):
         arrivals = refs[:n_in]
-        stay, y_part, z_mask, codes, x_pool, y_acc = refs[n_in:]
+        stay, y_part, z_mask, own_mask, codes, x_pool, y_acc = refs[n_in:]
         x_swapped, z_swapped, y_flip = swapped_of(x_axis), swapped_of(z_axis), flip_of(y_axis)
         for place in range(2 * CAP_X):
             ref, base = half(arrivals, place // CAP_X, x_rows)
@@ -252,7 +272,10 @@
 
         y_acc[...] = jnp.zeros(ACC, F32)
 
-        @pl.loop(0, blocks // 8)
+        for b in range(blocks):
+            own_mask[b : b + 1, :] = jnp.full((1, LANES), (codes[b] == 0).astype(F32))
+
+        @pl.loop(0, early // 8)
         def _(step):
             slabs = []
             for i in range(8):
@@ -300,15 +323,27 @@
     return kernel
 
 
-def make_stay(fields, n_in):
+def make_stay(fields, blocks, early, n_in):
     rows = packed_rows(fields, CAP_Z)
 
-    def kernel(stay, z_mask, *refs):
-        arrivals, out = refs[:n_in], refs[n_in]
+    def kernel(stay, z_mask, own_mask, pool, *refs):
+        arrivals, out, acc = refs[:n_in], refs[n_in], refs[n_in + 1]
         slabs = [
             (z_slab(arrivals, z_mask, 0, place, rows, fields), fields) for place in range(2 * CAP_Z)
         ]
-        put_sums(out, 0, stay[...] + binned(slabs), fields)
+        acc[...] = stay[...] + binned(slabs)
+        row = lax.broadcasted_iota(jnp.int32, (SLAB, LANES), 0)
+
+        @pl.loop(early // 8, blocks // 8)
+        def _(step):
+            slabs = []
+            for i in range(8):
+                b = step * 8 + i
+                keep = own_mask[pl.ds(b, 1), :]
+                slabs.append((pool[b] * jnp.where(row == fields, 1.0, keep), fields))
+            acc[...] += binned(slabs)
+
+        put_sums(out, 0, acc[...], fields)
 
     return kernel
 
@@ -348,17 +383,22 @@
     )
 
     def x_out(*refs):
-        x_out_kernel("gx", fields, *refs)
-
-    out = pl.pallas_call(
+        x_out_kernel("gx", *refs)
+
+    *out, f_in, s_in, l_in, c_in = pl.pallas_call(
         x_out,
-        out_shape=x_bufs,
-        in_specs=[SMEM] * 2 + [VMEM] * 4,
-        out_specs=[VMEM] * len(x_bufs),
+        out_shape=x_bufs + [jax.ShapeDtypeStruct(d.shape, d.dtype) for d in data],
+        in_specs=[HBM] * 6,
+        out_specs=[VMEM] * (len(x_bufs) + 4),
+        scratch_shapes=[
+            pltpu.SMEM(block_counts.shape, jnp.int32),
+            pltpu.SMEM(block_lists.shape, jnp.int32),
+            pltpu.SemaphoreType.DMA((5 + CHUNKS,)),
+        ],
         compiler_params=params(8),
         cost_estimate=cost(1 << 16, 1 << 20),
         name="x_out",
-    )(*lists, *data)
+    )(*(pltpu.with_memory_space_constraint(a, pltpu.HBM) for a in lists + data))
     x_in = exchange("gx", out)
 
     def pool_body(*refs):
@@ -376,7 +416,7 @@
         compiler_params=params(8),
         cost_estimate=cost(1 << 22, 1 << 20),
         name="pool",
-    )(*lists, *data)
+    )(*lists, f_in, s_in, l_in, c_in)
 
     out = pl.pallas_call(
         make_z_out(fields, len(x_in)),
@@ -389,11 +429,12 @@
     )(z_own, z_pick, *x_in)
     z_in = exchange("gz", out)
 
-    stay, y_part, z_mask = pl.pallas_call(
-        make_bin(fields, blocks, ("gx", "gz", "gy"), len(x_in)),
-        out_shape=[shape(*ACC), shape(2, *ACC), shape(3, 16, LANES)],
+    early = blocks // 32 * 8
+    stay, y_part, z_mask, own_mask = pl.pallas_call(
+        make_bin(fields, blocks, early, ("gx", "gz", "gy"), len(x_in)),
+        out_shape=[shape(*ACC), shape(2, *ACC), shape(3, 16, LANES), shape(blocks, LANES)],
         in_specs=[SMEM] * 2 + [VMEM] * (1 + len(x_in)),
-        out_specs=[VMEM] * 3,
+        out_specs=[VMEM] * 4,
         scratch_shapes=[
             pltpu.SMEM((blocks + 2 * CAP_X + 2 * CAP_Z + 1,), jnp.int32),
             pltpu.VMEM((2 * CAP_X, SLAB, LANES), F32),
@@ -416,14 +457,15 @@
     y_in = exchange("gy", out)
 
     stay = pl.pallas_call(
-        make_stay(fields, len(z_in)),
+        make_stay(fields, blocks, early, len(z_in)),
         out_shape=shape(y_rows, LANES),
-        in_specs=[VMEM] * (2 + len(z_in)),
+        in_specs=[VMEM] * (4 + len(z_in)),
         out_specs=VMEM,
-        compiler_params=params(8),
-        cost_estimate=cost(1 << 22, 1 << 19),
-        name="bin_z",
-    )(stay, z_mask, *z_in)
+        scratch_shapes=[pltpu.VMEM(ACC, F32)],
+        compiler_params=params(8),
+        cost_estimate=cost(1 << 26, 1 << 19),
+        name="bin_stay",
+    )(stay, z_mask, own_mask, pool, *z_in)
 
     return pl.pallas_call(
         make_final(fields, len(y_in)),

time: 25.5 us -> 22 us (0.86)
  local copies, waits for them, and re-layouts: 4.07 us -> 0.67 us
  waiting for transfers between devices: 4.63 us -> 3.66 us
  Pallas kernels: 7.03 us -> 7.88 us
    unnamed x12 -> x4, local copies, waits for them, and re-layouts: 4.07 us -> 0.67 us
    ppermute x2, waiting for transfers between devices: 2.83 us -> 0.3 us  [exchange(): lax.ppermute(bufs[0], axis, first)]
    ppermute x1, waiting for transfers between devices: 0.01 us -> 1.38 us  [exchange(): return [lax.ppermute(bufs[0], axis, [(0, 1), (1, 0)])]]
    pallas_call x3, Pallas kernels: 4.93 us -> 5.79 us  [the longest x1 2.39 us: per_device(): pl.pallas_call(make_bin(fields, blocks, early, ('gx', 'gz', 'gy'), len(x_...]
  transfers between devices with their start and end apart: 5 -> 5, of which waited for: 3 -> 3; matrix products, arithmetic and copies ran while one was open for 0% -> 0% of each run, Pallas kernels for 21% -> 24%
where the time goes in v2:
time: 22 us; the launch traced here: 21.8 us
  starting transfers between devices  9.55 us (43%)
  Pallas kernels  7.88 us (36%)
  waiting for transfers between devices  3.66 us (17%)
  local copies, waits for them, and re-layouts  0.67 us (3%)
    ppermute x2, starting transfers between devices, exchange(): lax.ppermute(bufs[0], axis, first)  6.36 us
    ppermute x1, starting transfers between devices, exchange(): return [lax.ppermute(bufs[0], axis, [(0, 1), (1, 0)])]  2.51 us
    pallas_call x1, Pallas kernels, per_device(): pl.pallas_call(make_bin(fields, blocks, early, ('gx', 'gz', 'gy'), len(x_...  2.39 us
    pallas_call x1, Pallas kernels, per_device(): pl.pallas_call(make_stay(fields, blocks, early, len(z_in)), out_shape=sha...  2 us
    ppermute x2, waiting for transfers between devices, exchange(): lax.ppermute(bufs[1], axis, second)  1.98 us
    pallas_call x1, Pallas kernels, per_device(): pl.pallas_call(x_out, out_shape=x_bufs + [jax.ShapeDtypeStruct(d.shape, d...  1.4 us
    ppermute x1, waiting for transfers between devices, exchange(): return [lax.ppermute(bufs[0], axis, [(0, 1), (1, 0)])]  1.38 us
    pallas_call x1, Pallas kernels, per_device(): pl.pallas_call(pool_body, out_shape=[shape(blocks, SLAB, LANES), shape(2...  0.84 us
  transfers between devices with their start and end apart: 5, of which 3 were waited for; matrix products, arithmetic and copies ran while one was open for 0% of the time, Pallas kernels for 24%

profile of v2, /device:TPU:0, one launch (start us, length us, event | category | flops | bytes accessed | tf_op | source)
XLA Modules:
  0.0 21.8 jit_solution(14572594240835133893)
XLA Ops:
  0.0 1.4 %x_out.1 = (f32[128,128]{1,0:T(8,128)S(1)}, f32[128,128]{1,0:T(8,128)S(1)}, f32[20,8192]{1,0:T(8,128)S(1)}, f32[64,128]{1,0:T(8,128)S(1)}, s32[64,128]{1,0:T(8,128)S(1)}, /*index=5*/s32[64,128]{1,0:T(8,128)S(1)}) custom-call(s32[1,6]{1,0:T(1,128)} %number.1, s32[1,48]{1,0:T(1,128)} %entries.1, f32[20,8192]{1,0:T(8,128)} %refs_2_.1, f32[64,128]{1,0:T(8,128)} %bitcast.3, ...), custom_call_target="tpu_custom_call" | custom-call | flops 65536 | bytes 1048576 | tf_op jit(solution)/shard_map/x_out/pallas_call | solution.py:388
  1.4 2.5 %collective-permute-start = (f32[128,128]{1,0:T(8,128)S(1)}, f32[128,128]{1,0:T(8,128)S(1)}, u32[]{:S(2)}, u32[]{:S(2)}) collective-permute-start(f32[128,128]{1,0:T(8,128)S(1)} %get-tuple-element.25), channel_id=1, source_target_pairs={{0,24},{8,16},{16,8},{24,0},{1,25},{9,17},{17,9},{25,1},{2,26},{10... | collective-permute-start | bytes 196616 | tf_op jit(solution)/shard_map/ppermute | solution.py:54
  3.9 0.7 %collective-permute-start.1 = (f32[128,128]{1,0:T(8,128)S(1)}, f32[128,128]{1,0:T(8,128)S(1)}, u32[]{:S(2)}, u32[]{:S(2)}) collective-permute-start(f32[128,128]{1,0:T(8,128)S(1)} %get-tuple-element.26), channel_id=1, source_target_pairs={{0,8},{8,0},{16,24},{24,16},{1,9},{9,1},{17,25},{25,17},{2,10},{10... | collective-permute-start | bytes 196616 | tf_op jit(solution)/shard_map/ppermute | solution.py:54
  4.6 0.0 copy-start
  4.6 0.0 copy-start.1
  4.6 0.7 %copy-done = s32[1,6]{1,0:T(1,128)S(1)} copy-done((s32[1,6]{1,0:T(1,128)S(1)}, s32[1,6]{1,0:T(1,128)}, u32[]{:S(2)}) %copy-start) | copy-done | bytes 48
  5.2 0.0 copy-done.1
  5.2 0.8 %pool.1 = (f32[64,24,128]{2,1,0:T(8,128)S(1)}, f32[12,24,128]{2,1,0:T(8,128)S(1)}, f32[12,16,128]{2,1,0:T(8,128)S(1)}) custom-call(s32[1,6]{1,0:T(1,128)S(1)} %copy-done, s32[1,48]{1,0:T(1,128)S(1)} %copy-done.1, f32[20,8192]{1,0:T(8,128)S(1)} %get-tuple-element.20.refs_2_, f32[64,128]{1,0:T(8,128)S(1)} %get-tuple-element.21.refs_3_, ...), custom_call_target="tpu_custom_call" | custom-call | flops 4194304 | bytes 1048576 | tf_op jit(solution)/shard_map/pool/pallas_call | solution.py:407
  6.1 0.3 %collective-permute-done.refs_0_ = f32[128,128]{1,0:T(8,128)S(1)} collective-permute-done((f32[128,128]{1,0:T(8,128)S(1)}, f32[128,128]{1,0:T(8,128)S(1)}, u32[]{:S(2)}, u32[]{:S(2)}) %collective-permute-start) | collective-permute-done | bytes 65568 | tf_op jit(solution)/shard_map/ppermute | solution.py:54
  6.4 0.0 collective-permute-done.1.refs_1_
  6.4 0.1 z_out.1
  6.5 2.5 %collective-permute-start.2 = (f32[256,128]{1,0:T(8,128)S(1)}, f32[256,128]{1,0:T(8,128)S(1)}, u32[]{:S(2)}, u32[]{:S(2)}) collective-permute-start(f32[256,128]{1,0:T(8,128)S(1)} %z_out.1), channel_id=1, source_target_pairs={{0,1},{1,0},{2,3},{3,2},{4,5},{5,4},{6,7},{7,6},{8,9},{9,8},{10,11... | collective-permute-start | bytes 393224 | tf_op jit(solution)/shard_map/ppermute | solution.py:47
  9.0 2.4 %bin_held.1 = (f32[192,128]{1,0:T(8,128)S(1)}, f32[2,192,128]{2,1,0:T(8,128)S(1)}, f32[3,16,128]{2,1,0:T(8,128)S(1)}, f32[64,128]{1,0:T(8,128)S(1)}) custom-call(s32[1,6]{1,0:T(1,128)S(1)} %copy-done, s32[1,48]{1,0:T(1,128)S(1)} %copy-done.1, f32[64,24,128]{2,1,0:T(8,128)S(1)} %get-tuple-element.24.pool, f32[128,128]{1,0:T(8,128)S(1)} %collective-permute-done.refs_0_, ...), custom_call_target="tpu_custom_call" | custom-call | flops 134217728 | bytes 1048576 | tf_op jit(solution)/shard_map/bin_held/pallas_call | solution.py:433
  11.4 1.4 %collective-permute-done.2.refs_0_ = f32[256,128]{1,0:T(8,128)S(1)} collective-permute-done((f32[256,128]{1,0:T(8,128)S(1)}, f32[256,128]{1,0:T(8,128)S(1)}, u32[]{:S(2)}, u32[]{:S(2)}) %collective-permute-start.2) | collective-permute-done | bytes 131104 | tf_op jit(solution)/shard_map/ppermute | solution.py:47
  12.8 0.5 %y_out.1 = (f32[80,128]{1,0:T(8,128)S(1)}, f32[80,128]{1,0:T(8,128)S(1)}) custom-call(f32[2,192,128]{2,1,0:T(8,128)S(1)} %get-tuple-element.32.y_part, f32[3,16,128]{2,1,0:T(8,128)S(1)} %get-tuple-element.28.z_mask, f32[256,128]{1,0:T(8,128)S(1)} %collective-permute-done.2.refs_0_), custom_call_target="tpu_custom_call" | custom-call | flops 1048576 | bytes 524288 | tf_op jit(solution)/shard_map/y_out/pallas_call | solution.py:448
  13.3 3.9 %collective-permute-start.3 = (f32[80,128]{1,0:T(8,128)S(1)}, f32[80,128]{1,0:T(8,128)S(1)}, u32[]{:S(2)}, u32[]{:S(2)}) collective-permute-start(f32[80,128]{1,0:T(8,128)S(1)} %get-tuple-element.33), channel_id=1, source_target_pairs={{0,6},{2,4},{4,2},{6,0},{1,7},{3,5},{5,3},{7,1},{8,14},{10,12},{12... | collective-permute-start | bytes 122888 | tf_op jit(solution)/shard_map/ppermute | solution.py:54
  17.2 0.0 collective-permute-start.4
  17.2 2.0 %bin_stay.1.stay = f32[80,128]{1,0:T(8,128)S(1)} custom-call(f32[192,128]{1,0:T(8,128)S(1)} %get-tuple-element.27.stay, f32[3,16,128]{2,1,0:T(8,128)S(1)} %get-tuple-element.28.z_mask, f32[64,128]{1,0:T(8,128)S(1)} %get-tuple-element.29.own_mask, f32[64,24,128]{2,1,0:T(8,128)S(1)} %get-tuple-element.24.pool, f32[256,128]{1,0:T(8,128)S(1)} %collective-permute-done.2.refs_0_), custom_call_target="tpu_custom_call" | custom-call | flops 67108864 | bytes 524288 | tf_op jit(solution)/shard_map/bin_stay/pallas_call | solution.py:459
  19.2 0.0 collective-permute-done.3.refs_0_
  19.2 2.0 %collective-permute-done.4.refs_1_ = f32[80,128]{1,0:T(8,128)S(1)} collective-permute-done((f32[80,128]{1,0:T(8,128)S(1)}, f32[80,128]{1,0:T(8,128)S(1)}, u32[]{:S(2)}, u32[]{:S(2)}) %collective-permute-start.4) | collective-permute-done | bytes 40992 | tf_op jit(solution)/shard_map/ppermute | solution.py:54
  21.2 0.6 %final.1 = f32[20,512]{1,0:T(8,128)} custom-call(f32[80,128]{1,0:T(8,128)S(1)} %bin_stay.1.stay, f32[80,128]{1,0:T(8,128)S(1)} %collective-permute-done.3.refs_0_, f32[80,128]{1,0:T(8,128)S(1)} %collective-permute-done.4.refs_1_), custom_call_target="tpu_custom_call" | custom-call | flops 65536 | bytes 131072 | tf_op jit(solution)/shard_map/final/pallas_call | solution.py:470
Async XLA Ops:
  1.4 5.0 %collective-permute-start = (f32[128,128]{1,0:T(8,128)S(1)}, f32[128,128]{1,0:T(8,128)S(1)}, u32[]{:S(2)}, u32[]{:S(2)}) collective-permute-start(f32[128,128]{1,0:T(8,128)S(1)} %get-tuple-element.25), channel_id=1, source_target_pairs={{0,24},{8,16},{16,8},{24,0},{1,25},{9,17},{17,9},{25,1},{2,26},{10... | collective-permute-start | bytes 196616 | tf_op jit(solution)/shard_map/ppermute | solution.py:54
  3.9 2.5 %collective-permute-start.1 = (f32[128,128]{1,0:T(8,128)S(1)}, f32[128,128]{1,0:T(8,128)S(1)}, u32[]{:S(2)}, u32[]{:S(2)}) collective-permute-start(f32[128,128]{1,0:T(8,128)S(1)} %get-tuple-element.26), channel_id=1, source_target_pairs={{0,8},{8,0},{16,24},{24,16},{1,9},{9,1},{17,25},{25,17},{2,10},{10... | collective-permute-start | bytes 196616 | tf_op jit(solution)/shard_map/ppermute | solution.py:54
  4.6 0.7 %copy-start = (s32[1,6]{1,0:T(1,128)S(1)}, s32[1,6]{1,0:T(1,128)}, u32[]{:S(2)}) copy-start(s32[1,6]{1,0:T(1,128)} %number.1) | copy-start | bytes 76
  4.6 0.7 %copy-start.1 = (s32[1,48]{1,0:T(1,128)S(1)}, s32[1,48]{1,0:T(1,128)}, u32[]{:S(2)}) copy-start(s32[1,48]{1,0:T(1,128)} %entries.1) | copy-start | bytes 580
  6.5 6.3 %collective-permute-start.2 = (f32[256,128]{1,0:T(8,128)S(1)}, f32[256,128]{1,0:T(8,128)S(1)}, u32[]{:S(2)}, u32[]{:S(2)}) collective-permute-start(f32[256,128]{1,0:T(8,128)S(1)} %z_out.1), channel_id=1, source_target_pairs={{0,1},{1,0},{2,3},{3,2},{4,5},{5,4},{6,7},{7,6},{8,9},{9,8},{10,11... | collective-permute-start | bytes 393224 | tf_op jit(solution)/shard_map/ppermute | solution.py:47
  13.3 5.9 %collective-permute-start.3 = (f32[80,128]{1,0:T(8,128)S(1)}, f32[80,128]{1,0:T(8,128)S(1)}, u32[]{:S(2)}, u32[]{:S(2)}) collective-permute-start(f32[80,128]{1,0:T(8,128)S(1)} %get-tuple-element.33), channel_id=1, source_target_pairs={{0,6},{2,4},{4,2},{6,0},{1,7},{3,5},{5,3},{7,1},{8,14},{10,12},{12... | collective-permute-start | bytes 122888 | tf_op jit(solution)/shard_map/ppermute | solution.py:54
  17.2 4.0 %collective-permute-start.4 = (f32[80,128]{1,0:T(8,128)S(1)}, f32[80,128]{1,0:T(8,128)S(1)}, u32[]{:S(2)}, u32[]{:S(2)}) collective-permute-start(f32[80,128]{1,0:T(8,128)S(1)} %get-tuple-element.34), channel_id=1, source_target_pairs={{0,2},{2,0},{4,6},{6,4},{1,3},{3,1},{5,7},{7,5},{8,10},{10,8},{12,... | collective-permute-start | bytes 122888 | tf_op jit(solution)/shard_map/ppermute | solution.py:54

commit v3 on v2

--- a/solution.py
+++ b/solution.py
@@ -18,7 +18,7 @@
 VMEM = pl.BlockSpec(memory_space=pltpu.VMEM)
 SMEM = pl.BlockSpec(memory_space=pltpu.SMEM)
 HBM = pl.BlockSpec(memory_space=pltpu.HBM)
-CHUNKS = 4
+CHUNKS = 1
 
 
 def params(mib):
@@ -29,28 +29,38 @@
     return pl.CostEstimate(flops=flops, bytes_accessed=nbytes, transcendentals=0)
 
 
-def pairwise(n):
-    return n > 2 and n % 2 == 0
+ORDER = {"gx": "up", "gy": "up", "gz": "down"}
+
+
+def order_of(axis):
+    n = lax.axis_size(axis)
+    if n == 2:
+        return "down"
+    return ORDER[axis] if n % 2 == 0 or ORDER[axis] in ("up", "down") else "down"
 
 
 def flip_of(axis):
-    return lax.axis_index(axis) % 2 if pairwise(lax.axis_size(axis)) else 0
+    order = order_of(axis)
+    if order in ("up", "down"):
+        return int(order == "up")
+    parity = lax.axis_index(axis) % 2
+    return parity if order == "odd" else 1 - parity
 
 
 def swapped_of(axis):
-    return lax.axis_index(axis) % 2 if pairwise(lax.axis_size(axis)) else 1
+    order = order_of(axis)
+    return 1 - flip_of(axis) if order in ("up", "down") else flip_of(axis)
 
 
 def exchange(axis, bufs):
     n = lax.axis_size(axis)
+    up, down = [(i, (i + 1) % n) for i in range(n)], [(i, (i - 1) % n) for i in range(n)]
     if n == 2:
-        return [lax.ppermute(bufs[0], axis, [(0, 1), (1, 0)])]
-    if pairwise(n):
-        first = [(i, (i + 1) % n if i % 2 else (i - 1) % n) for i in range(n)]
-        second = [(i, (i - 1) % n if i % 2 else (i + 1) % n) for i in range(n)]
-    else:
-        first = [(i, (i - 1) % n) for i in range(n)]
-        second = [(i, (i + 1) % n) for i in range(n)]
+        return [lax.ppermute(bufs[0], axis, up)]
+    odd = [up[i] if i % 2 else down[i] for i in range(n)]
+    even = [down[i] if i % 2 else up[i] for i in range(n)]
+    pairs = {"up": (up, down), "down": (down, up), "odd": (odd, even), "even": (even, odd)}
+    first, second = pairs[order_of(axis)]
     return [lax.ppermute(bufs[0], axis, first), lax.ppermute(bufs[1], axis, second)]
 
 
@@ -151,7 +161,7 @@
     flip = flip_of(axis)
     rows = packed_rows(fields, CAP_X)
     for side in range(2):
-        way = flip if side == 0 else 1 - flip
+        way = side ^ flip
         ref, base = half(outs, side, rows)
         for j in range(CAP_X):
             entry = entries[0, way * CAP_X + j]
@@ -178,7 +188,7 @@
     flip = flip_of(z_axis)
     swapped = swapped_of(x_axis)
     for side in range(2):
-        way = flip if side == 0 else 1 - flip
+        way = side ^ flip
         for j in range(CAP_Z):
             slot = side * CAP_Z + j
             valid = j < number[0, 2 + way]
@@ -243,7 +253,7 @@
             for way in range(2):
                 for j in range(cap):
                     valid = j < number[0, 2 * section + way]
-                    code = 1 if section < 2 else 2 + (way if isinstance(y_flip, int) else way ^ y_flip)
+                    code = 1 if section < 2 else 2 + (way ^ y_flip)
                     codes[jnp.where(valid, spot(entries[0, at]), total)] = code
                     at += 1
 
@@ -255,7 +265,7 @@
 
         first = 2 * CAP_X + 2 * CAP_Z
         for side in range(2):
-            way = side if isinstance(y_flip, int) else side ^ y_flip
+            way = side ^ y_flip
 
             def one(j):
                 entry = spot(entries[0, first + way * CAP_Y + j])

time: 22 us -> 20 us (0.909)
  waiting for transfers between devices: 3.66 us -> 2.78 us
  starting transfers between devices: 9.55 us -> 8.7 us
    ppermute x2, starting transfers between devices: 6.36 us -> 2.75 us  [exchange(): lax.ppermute(bufs[0], axis, first)]
    ppermute x2, starting transfers between devices: 0.68 us -> 4.07 us  [exchange(): lax.ppermute(bufs[1], axis, second)]
    ppermute x2, waiting for transfers between devices: 1.98 us -> 0.89 us  [exchange(): lax.ppermute(bufs[1], axis, second)]
    ppermute x1, starting transfers between devices: 2.51 us -> 1.88 us  [exchange(): return [lax.ppermute(bufs[0], axis, up)]]
    ppermute x2, waiting for transfers between devices: 0.3 us -> 0.56 us  [exchange(): lax.ppermute(bufs[0], axis, first)]
  transfers between devices with their start and end apart: 5 -> 5, of which waited for: 3 -> 5; matrix products, arithmetic and copies ran while one was open for 0% -> 0% of each run, Pallas kernels for 24% -> 26%
where the time goes in v3:
time: 20 us; the launch traced here: 19.9 us
  starting transfers between devices  8.7 us (43%)
  Pallas kernels  7.67 us (38%)
  waiting for transfers between devices  2.78 us (14%)
  local copies, waits for them, and re-layouts  0.67 us (3%)
    ppermute x2, starting transfers between devices, exchange(): lax.ppermute(bufs[1], axis, second)  4.07 us
    ppermute x2, starting transfers between devices, exchange(): lax.ppermute(bufs[0], axis, first)  2.75 us
    pallas_call x1, Pallas kernels, per_device(): pl.pallas_call(make_bin(fields, blocks, early, ('gx', 'gz', 'gy'), len(x_...  2.29 us
    pallas_call x1, Pallas kernels, per_device(): pl.pallas_call(make_stay(fields, blocks, early, len(z_in)), out_shape=sha...  2 us
    ppermute x1, starting transfers between devices, exchange(): return [lax.ppermute(bufs[0], axis, up)]  1.88 us
    ppermute x1, waiting for transfers between devices, exchange(): return [lax.ppermute(bufs[0], axis, up)]  1.33 us
    pallas_call x1, Pallas kernels, per_device(): pl.pallas_call(x_out, out_shape=x_bufs + [jax.ShapeDtypeStruct(d.shape, d...  1.29 us
    ppermute x2, waiting for transfers between devices, exchange(): lax.ppermute(bufs[1], axis, second)  0.89 us
  transfers between devices with their start and end apart: 5, of which 5 were waited for; matrix products, arithmetic and copies ran while one was open for 0% of the time, Pallas kernels for 26%

profile of v3, /device:TPU:0, one launch (start us, length us, event | category | flops | bytes accessed | tf_op | source)
XLA Modules:
  0.0 19.9 jit_solution(138485618817037147)
XLA Ops:
  0.0 1.3 %x_out.1 = (f32[128,128]{1,0:T(8,128)S(1)}, f32[128,128]{1,0:T(8,128)S(1)}, f32[20,8192]{1,0:T(8,128)S(1)}, f32[64,128]{1,0:T(8,128)S(1)}, s32[64,128]{1,0:T(8,128)S(1)}, /*index=5*/s32[64,128]{1,0:T(8,128)S(1)}) custom-call(s32[1,6]{1,0:T(1,128)} %number.1, s32[1,48]{1,0:T(1,128)} %entries.1, f32[20,8192]{1,0:T(8,128)} %refs_2_.1, f32[64,128]{1,0:T(8,128)} %bitcast.3, ...), custom_call_target="tpu_custom_call" | custom-call | flops 65536 | bytes 1048576 | tf_op jit(solution)/shard_map/x_out/pallas_call | solution.py:398
  1.3 0.5 %collective-permute-start = (f32[128,128]{1,0:T(8,128)S(1)}, f32[128,128]{1,0:T(8,128)S(1)}, u32[]{:S(2)}, u32[]{:S(2)}) collective-permute-start(f32[128,128]{1,0:T(8,128)S(1)} %get-tuple-element.25), channel_id=1, source_target_pairs={{0,8},{8,16},{16,24},{24,0},{1,9},{9,17},{17,25},{25,1},{2,10},{10... | collective-permute-start | bytes 196616 | tf_op jit(solution)/shard_map/ppermute | solution.py:64
  1.8 2.0 %collective-permute-start.1 = (f32[128,128]{1,0:T(8,128)S(1)}, f32[128,128]{1,0:T(8,128)S(1)}, u32[]{:S(2)}, u32[]{:S(2)}) collective-permute-start(f32[128,128]{1,0:T(8,128)S(1)} %get-tuple-element.26), channel_id=1, source_target_pairs={{0,24},{8,0},{16,8},{24,16},{1,25},{9,1},{17,9},{25,17},{2,26},{10... | collective-permute-start | bytes 196616 | tf_op jit(solution)/shard_map/ppermute | solution.py:64
  3.8 0.0 copy-start
  3.8 0.0 copy-start.1
  3.8 0.7 %copy-done = s32[1,6]{1,0:T(1,128)S(1)} copy-done((s32[1,6]{1,0:T(1,128)S(1)}, s32[1,6]{1,0:T(1,128)}, u32[]{:S(2)}) %copy-start) | copy-done | bytes 48
  4.5 0.0 copy-done.1
  4.5 0.8 %pool.1 = (f32[64,24,128]{2,1,0:T(8,128)S(1)}, f32[12,24,128]{2,1,0:T(8,128)S(1)}, f32[12,16,128]{2,1,0:T(8,128)S(1)}) custom-call(s32[1,6]{1,0:T(1,128)S(1)} %copy-done, s32[1,48]{1,0:T(1,128)S(1)} %copy-done.1, f32[20,8192]{1,0:T(8,128)S(1)} %get-tuple-element.20.refs_2_, f32[64,128]{1,0:T(8,128)S(1)} %get-tuple-element.21.refs_3_, ...), custom_call_target="tpu_custom_call" | custom-call | flops 4194304 | bytes 1048576 | tf_op jit(solution)/shard_map/pool/pallas_call | solution.py:417
  5.3 0.4 %collective-permute-done.refs_0_ = f32[128,128]{1,0:T(8,128)S(1)} collective-permute-done((f32[128,128]{1,0:T(8,128)S(1)}, f32[128,128]{1,0:T(8,128)S(1)}, u32[]{:S(2)}, u32[]{:S(2)}) %collective-permute-start) | collective-permute-done | bytes 65568 | tf_op jit(solution)/shard_map/ppermute | solution.py:64
  5.7 0.5 %collective-permute-done.1.refs_1_ = f32[128,128]{1,0:T(8,128)S(1)} collective-permute-done((f32[128,128]{1,0:T(8,128)S(1)}, f32[128,128]{1,0:T(8,128)S(1)}, u32[]{:S(2)}, u32[]{:S(2)}) %collective-permute-start.1) | collective-permute-done | bytes 65568 | tf_op jit(solution)/shard_map/ppermute | solution.py:64
  6.2 0.1 z_out.1
  6.4 1.9 %collective-permute-start.2 = (f32[256,128]{1,0:T(8,128)S(1)}, f32[256,128]{1,0:T(8,128)S(1)}, u32[]{:S(2)}, u32[]{:S(2)}) collective-permute-start(f32[256,128]{1,0:T(8,128)S(1)} %z_out.1), channel_id=1, source_target_pairs={{0,1},{1,0},{2,3},{3,2},{4,5},{5,4},{6,7},{7,6},{8,9},{9,8},{10,11... | collective-permute-start | bytes 393224 | tf_op jit(solution)/shard_map/ppermute | solution.py:59
  8.2 2.3 %bin_held.1 = (f32[192,128]{1,0:T(8,128)S(1)}, f32[2,192,128]{2,1,0:T(8,128)S(1)}, f32[3,16,128]{2,1,0:T(8,128)S(1)}, f32[64,128]{1,0:T(8,128)S(1)}) custom-call(s32[1,6]{1,0:T(1,128)S(1)} %copy-done, s32[1,48]{1,0:T(1,128)S(1)} %copy-done.1, f32[64,24,128]{2,1,0:T(8,128)S(1)} %get-tuple-element.24.pool, f32[128,128]{1,0:T(8,128)S(1)} %collective-permute-done.refs_0_, ...), custom_call_target="tpu_custom_call" | custom-call | flops 134217728 | bytes 1048576 | tf_op jit(solution)/shard_map/bin_held/pallas_call | solution.py:443
  10.5 1.3 %collective-permute-done.2.refs_0_ = f32[256,128]{1,0:T(8,128)S(1)} collective-permute-done((f32[256,128]{1,0:T(8,128)S(1)}, f32[256,128]{1,0:T(8,128)S(1)}, u32[]{:S(2)}, u32[]{:S(2)}) %collective-permute-start.2) | collective-permute-done | bytes 131104 | tf_op jit(solution)/shard_map/ppermute | solution.py:59
  11.9 0.5 %y_out.1 = (f32[80,128]{1,0:T(8,128)S(1)}, f32[80,128]{1,0:T(8,128)S(1)}) custom-call(f32[2,192,128]{2,1,0:T(8,128)S(1)} %get-tuple-element.32.y_part, f32[3,16,128]{2,1,0:T(8,128)S(1)} %get-tuple-element.28.z_mask, f32[256,128]{1,0:T(8,128)S(1)} %collective-permute-done.2.refs_0_), custom_call_target="tpu_custom_call" | custom-call | flops 1048576 | bytes 524288 | tf_op jit(solution)/shard_map/y_out/pallas_call | solution.py:458
  12.4 2.2 %collective-permute-start.3 = (f32[80,128]{1,0:T(8,128)S(1)}, f32[80,128]{1,0:T(8,128)S(1)}, u32[]{:S(2)}, u32[]{:S(2)}) collective-permute-start(f32[80,128]{1,0:T(8,128)S(1)} %get-tuple-element.33), channel_id=1, source_target_pairs={{0,2},{2,4},{4,6},{6,0},{1,3},{3,5},{5,7},{7,1},{8,10},{10,12},{12... | collective-permute-start | bytes 122888 | tf_op jit(solution)/shard_map/ppermute | solution.py:64
  14.6 2.1 %collective-permute-start.4 = (f32[80,128]{1,0:T(8,128)S(1)}, f32[80,128]{1,0:T(8,128)S(1)}, u32[]{:S(2)}, u32[]{:S(2)}) collective-permute-start(f32[80,128]{1,0:T(8,128)S(1)} %get-tuple-element.34), channel_id=1, source_target_pairs={{0,6},{2,0},{4,2},{6,4},{1,7},{3,1},{5,3},{7,5},{8,14},{10,8},{12,... | collective-permute-start | bytes 122888 | tf_op jit(solution)/shard_map/ppermute | solution.py:64
  16.7 2.0 %bin_stay.1.stay = f32[80,128]{1,0:T(8,128)S(1)} custom-call(f32[192,128]{1,0:T(8,128)S(1)} %get-tuple-element.27.stay, f32[3,16,128]{2,1,0:T(8,128)S(1)} %get-tuple-element.28.z_mask, f32[64,128]{1,0:T(8,128)S(1)} %get-tuple-element.29.own_mask, f32[64,24,128]{2,1,0:T(8,128)S(1)} %get-tuple-element.24.pool, f32[256,128]{1,0:T(8,128)S(1)} %collective-permute-done.2.refs_0_), custom_call_target="tpu_custom_call" | custom-call | flops 67108864 | bytes 524288 | tf_op jit(solution)/shard_map/bin_stay/pallas_call | solution.py:469
  18.7 0.2 collective-permute-done.3.refs_0_
  18.9 0.4 %collective-permute-done.4.refs_1_ = f32[80,128]{1,0:T(8,128)S(1)} collective-permute-done((f32[80,128]{1,0:T(8,128)S(1)}, f32[80,128]{1,0:T(8,128)S(1)}, u32[]{:S(2)}, u32[]{:S(2)}) %collective-permute-start.4) | collective-permute-done | bytes 40992 | tf_op jit(solution)/shard_map/ppermute | solution.py:64
  19.2 0.6 %final.1 = f32[20,512]{1,0:T(8,128)} custom-call(f32[80,128]{1,0:T(8,128)S(1)} %bin_stay.1.stay, f32[80,128]{1,0:T(8,128)S(1)} %collective-permute-done.3.refs_0_, f32[80,128]{1,0:T(8,128)S(1)} %collective-permute-done.4.refs_1_), custom_call_target="tpu_custom_call" | custom-call | flops 65536 | bytes 131072 | tf_op jit(solution)/shard_map/final/pallas_call | solution.py:480
Async XLA Ops:
  1.3 4.4 %collective-permute-start = (f32[128,128]{1,0:T(8,128)S(1)}, f32[128,128]{1,0:T(8,128)S(1)}, u32[]{:S(2)}, u32[]{:S(2)}) collective-permute-start(f32[128,128]{1,0:T(8,128)S(1)} %get-tuple-element.25), channel_id=1, source_target_pairs={{0,8},{8,16},{16,24},{24,0},{1,9},{9,17},{17,25},{25,1},{2,10},{10... | collective-permute-start | bytes 196616 | tf_op jit(solution)/shard_map/ppermute | solution.py:64
  1.8 4.4 %collective-permute-start.1 = (f32[128,128]{1,0:T(8,128)S(1)}, f32[128,128]{1,0:T(8,128)S(1)}, u32[]{:S(2)}, u32[]{:S(2)}) collective-permute-start(f32[128,128]{1,0:T(8,128)S(1)} %get-tuple-element.26), channel_id=1, source_target_pairs={{0,24},{8,0},{16,8},{24,16},{1,25},{9,1},{17,9},{25,17},{2,26},{10... | collective-permute-start | bytes 196616 | tf_op jit(solution)/shard_map/ppermute | solution.py:64
  3.8 0.7 %copy-start = (s32[1,6]{1,0:T(1,128)S(1)}, s32[1,6]{1,0:T(1,128)}, u32[]{:S(2)}) copy-start(s32[1,6]{1,0:T(1,128)} %number.1) | copy-start | bytes 76
  3.8 0.7 %copy-start.1 = (s32[1,48]{1,0:T(1,128)S(1)}, s32[1,48]{1,0:T(1,128)}, u32[]{:S(2)}) copy-start(s32[1,48]{1,0:T(1,128)} %entries.1) | copy-start | bytes 580
  6.4 5.5 %collective-permute-start.2 = (f32[256,128]{1,0:T(8,128)S(1)}, f32[256,128]{1,0:T(8,128)S(1)}, u32[]{:S(2)}, u32[]{:S(2)}) collective-permute-start(f32[256,128]{1,0:T(8,128)S(1)} %z_out.1), channel_id=1, source_target_pairs={{0,1},{1,0},{2,3},{3,2},{4,5},{5,4},{6,7},{7,6},{8,9},{9,8},{10,11... | collective-permute-start | bytes 393224 | tf_op jit(solution)/shard_map/ppermute | solution.py:59
  12.4 6.5 %collective-permute-start.3 = (f32[80,128]{1,0:T(8,128)S(1)}, f32[80,128]{1,0:T(8,128)S(1)}, u32[]{:S(2)}, u32[]{:S(2)}) collective-permute-start(f32[80,128]{1,0:T(8,128)S(1)} %get-tuple-element.33), channel_id=1, source_target_pairs={{0,2},{2,4},{4,6},{6,0},{1,3},{3,5},{5,7},{7,1},{8,10},{10,12},{12... | collective-permute-start | bytes 122888 | tf_op jit(solution)/shard_map/ppermute | solution.py:64
  14.6 4.7 %collective-permute-start.4 = (f32[80,128]{1,0:T(8,128)S(1)}, f32[80,128]{1,0:T(8,128)S(1)}, u32[]{:S(2)}, u32[]{:S(2)}) collective-permute-start(f32[80,128]{1,0:T(8,128)S(1)} %get-tuple-element.34), channel_id=1, source_target_pairs={{0,6},{2,0},{4,2},{6,4},{1,7},{3,1},{5,3},{7,5},{8,14},{10,8},{12,... | collective-permute-start | bytes 122888 | tf_op jit(solution)/shard_map/ppermute | solution.py:64
